TPU v7x, 256 devices: a whole 4x4x8 slice. The times are simulated.
256 devices in a mesh: seq: 64 (over z, y, core), mix: 4 (over x).
Axes of the slice: x: 4, y: 4, z: 8, core: 2. Of those that a mesh axis runs over, the one named last changes fastest.
Arguments:
- tokens: bfloat16 [8, 16384, 512], P('mix', 'seq'), may hold values from -6 to 6
- log_forget_rate: bfloat16 [8, 16384, 16], P('mix', 'seq'), may hold values from -0.7 to 0, as said below
- w_x: bfloat16 [512, 1024], P(None, 'mix'), may hold values from -0.25 to 0.25
- w_z: bfloat16 [512, 1024], P(None, 'mix'), may hold values from -0.25 to 0.25
- w_bc: bfloat16 [512, 128], replicated, may hold values from -0.25 to 0.25
- conv_x: bfloat16 [4, 1024], P(None, 'mix'), may hold values from -3 to 3
- conv_bc: bfloat16 [4, 128], replicated, may hold values from -3 to 3
- skip: bfloat16 [16], P('mix'), may hold values from 0.5 to 2
- gain: bfloat16 [1024], P('mix'), may hold values from 0.099609375 to 1.8984375
- w_out: bfloat16 [1024, 512], P('mix'), may hold values from -0.1875 to 0.1875
Outputs:
- mixed: bfloat16 [8, 16384, 512], P('mix', 'seq')
Inputs may be any that keep to these rules, and one draw needn't show every extreme that they name: `log_forget_rate`: every entry is below zero.
All inputs are finite; a program needn't handle non-finite values.
Results may differ from a plain program's by a relative error of at most 0.012.
Values may be sent and summed in bfloat16 or wider, within the bound.
No kernel may reach another device: no remote copies, remote signals or barrier semaphores. Data moves between devices by JAX's collectives and lax.ppermute only.
A program may use at most 128 MiB of HBM per device.

v0:
```python
import jax
import jax.numpy as jnp
from jax import lax
from jax.experimental import pallas as pl
from jax.experimental.pallas import tpu as pltpu
from jax.sharding import Mesh
from jax.sharding import PartitionSpec as P


F32, BF16 = jnp.float32, jnp.bfloat16
CHIPS = ("seq_0", "seq_1")
SEQ = ("seq_0", "seq_1", "seq_2")
STATE = 64
CONV = 4
BLOCK = 128
LANES = 128
HALO = 16
SHARDS = 4
PART = 16


def dot(a, b):
    return jnp.dot(a, b, preferred_element_type=F32)


def iota(shape, axis):
    return lax.broadcasted_iota(jnp.int32, shape, axis)


def ones_where(mask):
    return jnp.where(mask, 1.0, 0.0).astype(BF16)


def hi_lo(value):
    high = value.astype(BF16)
    low = (value - high.astype(F32)).astype(BF16)
    return jnp.concatenate([high, low], axis=-1)


def lower_ones(size):
    return ones_where(iota((size, size), 0) >= iota((size, size), 1))


def spread(start, width):
    shape = (2 * LANES, width)
    return ones_where((iota(shape, 0) & (LANES - 1)) == ((iota(shape, 1) + start) >> 6))


def scale_of(rate):
    z = 2.0 * rate
    series = z * (
        1.0
        + z * (1 / 2 + z * (1 / 6 + z * (1 / 24 + z * (1 / 120 + z * (1 / 720)))))
    )
    return jnp.sqrt(jnp.maximum(-jnp.where(z > -0.25, series, jnp.exp(z) - 1.0), 0.0))


def silu(value):
    return value * jax.nn.sigmoid(value)


def conv_silu(halo_rows, rows, taps):
    rows = jnp.concatenate([halo_rows, rows], axis=0).astype(BF16).astype(F32)
    total = taps[CONV - 1 : CONV] * rows
    for back in range(1, CONV):
        total = total + taps[CONV - 1 - back : CONV - back] * pltpu.roll(rows, back, 0)
    return silu(total[HALO:]).astype(BF16)


def shard_states(weight, taps, r, at, tok_ref, halo_ref, tail_ref, bt_ref, xa_ref, msg_ref):
    wide = weight.shape[1]
    xa = conv_silu(dot(halo_ref[...], weight), dot(tok_ref[...], weight), taps)
    xa_ref[:, at : at + wide] = xa
    tail = dot(tail_ref[...], spread(r * wide, wide))
    state = dot(bt_ref[0:STATE, :], (xa.astype(F32) * tail).astype(BF16)).astype(BF16)
    for p in range(wide // LANES):
        for q in range(STATE // PART):
            at_piece = (r * (wide // LANES) + p) * (STATE // PART) + q
            msg_ref[at_piece, 0:PART] = state[q * PART : (q + 1) * PART, p * LANES : (p + 1) * LANES]


def decay_kernel(c_ref, x_ref, tokens_ref, log_ref, got_ref, got_log_ref, tok_ref, edge_ref, logp_ref, tail_ref, extra_ref):
    core, mine = c_ref[0], x_ref[0]
    heads, length = log_ref.shape[1:]
    here = pl.multiple_of(core * length, length)
    there = pl.multiple_of((1 - core) * length, length)
    tok_ref[pl.ds(here, length)] = tokens_ref[core]
    tok_ref[pl.ds(there, length)] = got_ref[core]
    edge_ref[...] = tok_ref[2 * length - HALO :]
    per = heads // SHARDS
    shape = (LANES, heads)
    rel = iota(shape, 0)
    source = per * ((mine - rel // per + SHARDS) & (SHARDS - 1)) + rel % per
    order = ones_where((iota(shape, 1) == source) & (rel < heads))
    a, b = log_ref[core], got_log_ref[core]
    logs = jnp.concatenate([jnp.where(core == 0, a, b), jnp.where(core == 0, b, a)], axis=1)
    rate = dot(order, logs).T
    logp = rate.astype(BF16)
    logp_ref[...] = logp
    cum = dot(lower_ones(2 * length), logp)
    total = cum[2 * length - 1 :]
    tail_ref[...] = hi_lo(jnp.exp(total - cum) * scale_of(rate))
    width = extra_ref.shape[1]
    total_x = dot(hi_lo(jnp.broadcast_to(total, (8, LANES))), spread(0, width))
    high = total_x.astype(BF16).astype(F32)
    row = iota((8, width), 0)
    extra_ref[...] = jnp.where(row == 0, high, jnp.where(row == 1, total_x - high, 0.0)).astype(BF16)


def own_kernel(
    tok_ref, halo_ref, tail_ref, extra_ref, wbc_ref, cbc_ref, w_ref, cx_ref,
    bc_ref, bt_ref, xa_ref, msg_ref,
):
    extra = extra_ref[...]
    parts = STATE // PART
    for j in range(extra.shape[1] // LANES):
        for q in range(parts):
            msg_ref[j * parts + q, PART : PART + 8] = extra[:, j * LANES : (j + 1) * LANES]
    taps = cbc_ref[...].astype(F32)
    bc = conv_silu(dot(halo_ref[...], wbc_ref[...]), dot(tok_ref[...], wbc_ref[...]), taps)
    bc_ref[...] = bc
    bt_ref[...] = bc.astype(F32).T.astype(BF16)
    shard_states(w_ref[...], cx_ref[...].astype(F32), 0, 0, tok_ref, halo_ref, tail_ref, bt_ref, xa_ref, msg_ref)


def others_kernel(c_ref, tok_ref, halo_ref, tail_ref, bt_ref, bc_ref, logp_ref, own_msg_ref, *rest):
    here, there = rest[0 : SHARDS - 1], rest[SHARDS - 1 : 2 * SHARDS - 2]
    xa_ref, msg_ref, seen_ref, w_ref = rest[2 * SHARDS - 2 :]
    core = c_ref[0]
    seen_ref[:, 0:LANES] = bc_ref[...]
    seen_ref[:, LANES:] = logp_ref[...]
    half, wide = w_ref.shape[0] // 2, w_ref.shape[1]
    msg_ref[...] = own_msg_ref[...]
    for r in range(1, SHARDS):
        a, b = here[r - 1][0:half], there[r - 1][0:half]
        w_ref[0:half] = jnp.where(core == 0, a, b)
        w_ref[half : 2 * half] = jnp.where(core == 0, b, a)
        taps = here[r - 1][half : half + 8].astype(F32)
        shard_states(w_ref[...], taps, r, (r - 1) * wide, tok_ref, halo_ref, tail_ref, bt_ref, xa_ref, msg_ref)


def scan_kernel(s_ref, out_ref):
    def step(k, carry):
        out_ref[k] = carry.astype(BF16)
        extra = s_ref[k, PART : PART + 8].astype(F32)
        return carry * jnp.exp(extra[0:1] + extra[1:2]) + s_ref[k, 0:PART].astype(F32)

    lax.fori_loop(0, s_ref.shape[0], step, jnp.zeros((PART, LANES), F32), unroll=8)


def intra_kernel(xa0_ref, xa1_ref, seen_ref, p0_ref, *rest):
    z_refs, y_ref = rest[:-1], rest[-1]
    length, wide = xa0_ref.shape
    depth = z_refs[0].shape[0] - 8
    blocks = length // BLOCK
    lower_block = lower_ones(BLOCK)
    keep = iota((BLOCK, BLOCK), 0) >= iota((BLOCK, BLOCK), 1)
    left = iota((BLOCK, LANES), 1) < LANES // 2
    bc = seen_ref[:, 0:LANES]
    bt = bc.astype(F32).T.astype(BF16)
    logp = seen_ref[:, LANES:]
    scale = scale_of(logp.astype(F32))
    scale_t = scale.T
    span = [slice(b * BLOCK, (b + 1) * BLOCK) for b in range(blocks)]
    cums = [dot(lower_block, logp[span[b]]) for b in range(blocks)]
    cums_t = [cum.T for cum in cums]
    reads = [bc[span[b]][:, STATE:] for b in range(blocks)]
    writes_t = [bt[0:STATE, b * BLOCK : (b + 1) * BLOCK] for b in range(blocks)]
    scores = [jnp.where(keep, dot(reads[b], writes_t[b]), 0.0) for b in range(blocks)]
    enter = [hi_lo(jnp.exp(cum)) for cum in cums]
    leave = [hi_lo(jnp.exp(cums[b][BLOCK - 1 :] - cums[b]) * scale[span[b]]) for b in range(blocks)]
    last = [hi_lo(jnp.broadcast_to(jnp.exp(cums[b][BLOCK - 1 :]), (8, LANES))) for b in range(blocks)]
    for j in range(SHARDS * wide // LANES):
        lanes = slice(j * LANES, (j + 1) * LANES)
        to_lanes = spread(j * LANES, LANES)
        r, at = divmod(j * LANES, wide)
        extra = p0_ref[...] if r == 0 else z_refs[r - 1][depth : depth + 8]
        skip = extra[1:2, at : at + LANES].astype(F32)
        state = None
        for b in range(blocks):
            if j * LANES < wide:
                xb = xa0_ref[span[b], lanes]
            else:
                xb = xa1_ref[span[b], j * LANES - wide : (j + 1) * LANES - wide]
            parts = []
            for h in (2 * j, 2 * j + 1):
                seg = cums[b][:, h : h + 1] - cums_t[b][h : h + 1, :]
                decay = jnp.exp(jnp.minimum(seg, 0.0))
                weights = decay * (scores[b] * scale_t[h : h + 1, span[b]])
                parts.append(weights.astype(BF16))
            zero = jnp.zeros_like(xb)
            split = jnp.concatenate([jnp.where(left, xb, zero), jnp.where(left, zero, xb)], axis=0)
            y = dot(jnp.concatenate(parts, axis=1), split) + skip * xb.astype(F32)
            if state is not None:
                y = y + dot(enter[b], to_lanes) * dot(reads[b], state.astype(BF16))
            if b + 1 < blocks:
                scaled = (xb.astype(F32) * dot(leave[b], to_lanes)).astype(BF16)
                fresh = dot(writes_t[b], scaled)
                state = fresh if state is None else fresh + dot(last[b], to_lanes)[0:1] * state
            y_ref[span[b], lanes] = y.astype(BF16)


def gate_kernel(c_ref, tok_ref, seen_ref, y_ref, wz0_ref, wo0_ref, p0_ref, *rest):
    here, there = rest[0 : SHARDS - 1], rest[SHARDS - 1 : 2 * SHARDS - 2]
    yg_ref, eg_ref, wo_ref, gain_ref, wz_ref = rest[2 * SHARDS - 2 :]
    core = c_ref[0]
    depth, wide = wz0_ref.shape
    half, q = depth // 2, wide // 2
    length = tok_ref.shape[0]
    wo_ref[0:wide] = wo0_ref[...]
    grow = hi_lo(jnp.exp(dot(lower_ones(length), seen_ref[:, LANES:])))
    for r in range(SHARDS):
        if r == 0:
            wz_ref[...] = wz0_ref[...]
            extra = p0_ref[...]
        else:
            a, b = here[r - 1], there[r - 1]
            wz_ref[0:half] = jnp.where(core == 0, a[0:half], b[0:half])
            wz_ref[half:depth] = jnp.where(core == 0, b[0:half], a[0:half])
            for s in range(2):
                part = slice(half + s * q, half + (s + 1) * q)
                lanes = slice(s * wide, (s + 1) * wide)
                wo_ref[r * wide : r * wide + q, lanes] = jnp.where(core == 0, a[part], b[part])
                wo_ref[r * wide + q : (r + 1) * wide, lanes] = jnp.where(core == 0, b[part], a[part])
            extra = a[2 * half : 2 * half + 8]
        lanes = slice(r * wide, (r + 1) * wide)
        gain_ref[:, lanes] = extra
        gate = silu(dot(tok_ref[...], wz_ref[...]).astype(BF16).astype(F32))
        yg_ref[:, lanes] = (y_ref[:, lanes].astype(F32) * gate).astype(BF16)
        eg_ref[:, lanes] = (dot(grow, spread(r * wide, wide)) * gate).astype(BF16)


def final_rows(start, back_ref, seen_ref, yg_ref, eg_ref, gain_ref, wo_ref, normed_ref):
    length, width = normed_ref.shape
    rows = pl.ds(pl.multiple_of(start, length), length)
    read = seen_ref[rows, STATE : 2 * STATE]
    shape = (2 * LANES, LANES)
    same_head = ones_where(((iota(shape, 0) & (LANES - 1)) >> 6) == (iota(shape, 1) >> 6))
    parts = STATE // PART
    for j in range(width // LANES):
        lanes = slice(j * LANES, (j + 1) * LANES)
        carry = jnp.concatenate([back_ref[j * parts + q] for q in range(parts)], axis=0)
        v = yg_ref[rows, lanes].astype(F32) + eg_ref[rows, lanes].astype(F32) * dot(read, carry)
        mean = dot(hi_lo(v * v), same_head) * (1.0 / 64.0)
        gain = gain_ref[0:1, lanes].astype(F32)
        normed_ref[:, lanes] = (v * lax.rsqrt(mean + 1e-05) * gain).astype(BF16)
    return dot(normed_ref[...], wo_ref[...]).astype(BF16)


def final_send_kernel(c_ref, back_ref, seen_ref, yg_ref, eg_ref, gain_ref, wo_ref, out_ref, normed_ref):
    start = (1 - c_ref[0]) * normed_ref.shape[0]
    out_ref[...] = final_rows(start, back_ref, seen_ref, yg_ref, eg_ref, gain_ref, wo_ref, normed_ref)


def final_own_kernel(c_ref, back_ref, seen_ref, yg_ref, eg_ref, gain_ref, wo_ref, out_ref, normed_ref):
    start = c_ref[0] * normed_ref.shape[0]
    out_ref[...] = final_rows(start, back_ref, seen_ref, yg_ref, eg_ref, gain_ref, wo_ref, normed_ref)


def join_kernel(c_ref, own_ref, got_ref, out_ref, sems):
    core = c_ref[0]
    copies = [
        pltpu.make_async_copy(own_ref, out_ref.at[core], sems.at[0]),
        pltpu.make_async_copy(got_ref, out_ref.at[1 - core], sems.at[1]),
    ]
    for copy in copies:
        copy.start()
    for copy in copies:
        copy.wait()


VMEM = pl.BlockSpec(memory_space=pltpu.VMEM)
SMEM = pl.BlockSpec(memory_space=pltpu.SMEM)
HBM = pl.BlockSpec(memory_space=pltpu.HBM)
ANY = pl.BlockSpec()


def call(kernel, outs, args, specs, out_specs=None, scratch=(), flops=0, mib=24):
    return pl.pallas_call(
        kernel,
        out_shape=[jax.ShapeDtypeStruct(shape, dtype) for shape, dtype in outs],
        in_specs=specs,
        out_specs=out_specs or [VMEM] * len(outs),
        scratch_shapes=list(scratch),
        compiler_params=pltpu.CompilerParams(vmem_limit_bytes=mib * 2**20),
        cost_estimate=pl.CostEstimate(flops=flops, bytes_accessed=2**20, transcendentals=0),
    )(*args)


def around(value, axis, steps):
    count = lax.axis_size(axis)
    return lax.ppermute(value, axis, [(k, (k + steps) % count) for k in range(count)])


def padded(value, above, rows, columns=None):
    columns = value.shape[1] if columns is None else columns
    return lax.pad(
        value, jnp.zeros((), value.dtype), [(above, rows - above - value.shape[0], 0), (0, columns - value.shape[1], 0)]
    )


def layer(tokens, log_forget_rate, w_x, w_z, w_bc, conv_x, conv_bc, skip, gain, w_out):
    core, across = lax.axis_index("seq_2"), lax.axis_index("mix")
    core_s, across_s = core.astype(jnp.int32)[None], across.astype(jnp.int32)[None]
    _, length, depth = tokens.shape
    wide = w_x.shape[1]
    width = wide * SHARDS
    half = depth // 2
    chips = lax.axis_size(CHIPS)
    both = 2 * length
    logs = jnp.swapaxes(log_forget_rate, 1, 2)
    parts = width // LANES * (STATE // PART)

    low = core == 0
    first = padded(jnp.where(low, w_x[:half], w_x[half:]), 0, half + 8) + padded(conv_x, half, half + 8)
    x_here = [around(first, "mix", r) for r in (2, 1, 3)]
    x_here = [x_here[1], x_here[0], x_here[2]]
    got = around(tokens, "seq_2", 1)
    got_log = around(logs, "seq_2", 1)
    tok, edge, logp, tail, extra = call(
        decay_kernel,
        [
            ((both, depth), BF16),
            ((HALO, depth), BF16),
            ((both, LANES), BF16),
            ((both, 2 * LANES), BF16),
            ((8, width), BF16),
        ],
        (core_s, across_s, tokens, logs, got, got_log),
        [SMEM, SMEM, ANY, ANY, VMEM, VMEM],
        flops=10**9,
    )
    halo = lax.ppermute(edge, CHIPS, [(k, k + 1) for k in range(chips - 1)])
    bc, bt, xa0, own_msg = call(
        own_kernel,
        [((both, 2 * STATE), BF16), ((2 * STATE, both), BF16), ((both, wide), BF16), ((parts, PART + 8, LANES), BF16)],
        (tok, halo, tail, extra, w_bc, conv_bc, w_x, conv_x),
        [VMEM] * 4 + [ANY] * 4,
        flops=10**9,
    )
    w_z, w_out, gain, skip, tok = lax.optimization_barrier((w_z, w_out, gain, skip, tok))
    p0 = padded(gain[None], 0, 8) + padded(jnp.repeat(skip, wide // skip.shape[0])[None], 1, 8)
    out_half = jnp.where(low, w_out[: wide // 2], w_out[wide // 2 :])
    rows = 2 * half + 8
    second = (
        padded(jnp.where(low, w_z[:half], w_z[half:]), 0, rows)
        + padded(out_half[:, :wide], half, rows)
        + padded(out_half[:, wide:], half + wide // 2, rows)
        + padded(p0, 2 * half, rows)
    )
    z_here = [around(second, "mix", r) for r in range(1, SHARDS)]

    (x_here, own_msg) = lax.optimization_barrier((x_here, own_msg))
    x_there = [around(part, "seq_2", 1) for part in x_here]
    xa1, msg, seen = call(
        others_kernel,
        [((both, width - wide), BF16), ((parts, PART + 8, LANES), BF16), ((both, 2 * LANES), BF16)],
        (core_s, tok, halo, tail, bt, bc, logp, own_msg, *x_here, *x_there),
        [SMEM] + [VMEM] * 13,
        scratch=[pltpu.VMEM((depth, wide), BF16)],
        flops=10**9,
    )
    arrived = lax.all_to_all(msg, CHIPS, 0, 0)
    (y,) = call(intra_kernel, [((both, width), BF16)], (xa0, xa1, seen, p0, *z_here), [VMEM] * 7, flops=2 * 10**9)
    (carries,) = call(scan_kernel, [((parts, PART, LANES), BF16)], (arrived,), [VMEM], flops=10**7)
    z_there = [around(part, "seq_2", 1) for part in z_here]
    back = lax.all_to_all(carries, CHIPS, 0, 0)
    y, back = lax.optimization_barrier((y, back))
    yg, eg, wo, gains = call(
        gate_kernel,
        [((both, width), BF16), ((both, width), BF16), ((width, depth), BF16), ((8, width), BF16)],
        (core_s, tok, seen, y, w_z, w_out, p0, *z_here, *z_there),
        [SMEM] + [ANY] * 12,
        scratch=[pltpu.VMEM((depth, wide), BF16)],
        flops=2 * 10**9,
    )
    ends = (core_s, back, seen, yg, eg, gains, wo)
    specs = [SMEM, VMEM, ANY, VMEM, VMEM, VMEM, VMEM]
    scratch = [pltpu.VMEM((length, width), BF16)]
    (away,) = call(final_send_kernel, [((length, depth), BF16)], ends, specs, scratch=scratch, flops=10**9)
    back_home = around(away, "seq_2", 1)
    (home,) = call(final_own_kernel, [((length, depth), BF16)], ends, specs, scratch=scratch, flops=10**9)
    (mixed,) = call(
        join_kernel,
        [((2, length, depth), BF16)],
        (core_s, home, back_home),
        [SMEM, VMEM, VMEM],
        out_specs=[HBM],
        scratch=[pltpu.SemaphoreType.DMA((2,))],
    )
    return mixed


def solution(mesh):
    finer = Mesh(
        mesh.devices.reshape(8, 4, 2, mesh.shape["mix"]), ("seq_0", "seq_1", "seq_2", "mix")
    )
    placed = (
        P("mix", SEQ, None),
        P("mix", SEQ, None),
        P(None, "mix"),
        P(None, "mix"),
        P(),
        P(None, "mix"),
        P(),
        P("mix"),
        P("mix"),
        P("mix", None),
    )
    return jax.shard_map(layer, mesh=finer, in_specs=placed, out_specs=P("mix", SEQ, None), check_vma=False)
```

profile of v0, /device:TPU:1, one launch (start us, length us, event | category | flops | bytes accessed | tf_op | source)
XLA Modules:
  0.0 83.4 jit_solution(15116844970248440629)
XLA Ops:
  0.0 3.2 %collective-permute-start = (bf16[2,256,512]{2,1,0:T(8,128)(2,1)}, bf16[2,256,512]{2,1,0:T(8,128)(2,1)S(1)}, u32[]{:S(2)}, u32[]{:S(2)}) collective-permute-start(bf16[2,256,512]{2,1,0:T(8,128)(2,1)} %tokens_ref.1), channel_id=1, source_target_pairs={{0,4},{4,0},{1,5},{5,1},{2,6},{6,2},{3,7},{7,3},{8,12},{12,8},{9,1... | collective-permute-start | bytes 1572872 | tf_op jit(solution)/shard_map/ppermute | solution.py:292
  3.2 1.0 %slice_select_fusion.2 = bf16[256,256]{1,0:T(8,128)(2,1)S(1)} fusion(bf16[512,256]{1,0:T(8,128)(2,1)} %w_ref.1, pred[]{:T(512)S(6)} %eq.3), kind=kLoop, calls=%fused_computation.4 | loop fusion | flops 65536 | bytes 393217 | tf_op jit(solution)/shard_map/jit(_where)/select_n | solution.py:315
  4.3 0.0 copy-start.6
  4.3 0.8 %collective-permute-start.5 = (bf16[264,256]{1,0:T(8,128)(2,1)S(1)}, bf16[264,256]{1,0:T(8,128)(2,1)S(1)}, u32[]{:S(2)}, u32[]{:S(2)}) collective-permute-start(bf16[264,256]{1,0:T(8,128)(2,1)S(1)} %pad_add_fusion.1), channel_id=1, source_target_pairs={{0,3},{1,0},{2,1},{3,2},{4,7},{5,4},{6,5},{7,6},{8,11},{9,8},{10,9... | collective-permute-start | bytes 405512 | tf_op jit(solution)/shard_map/ppermute | solution.py:292
  5.1 0.5 collective-permute-start.4
  5.7 0.6 collective-permute-start.3
  6.3 0.9 %shard_map.100 = (bf16[512,512]{1,0:T(8,128)(2,1)S(1)}, bf16[16,512]{1,0:T(8,128)(2,1)S(1)}, bf16[512,128]{1,0:T(8,128)(2,1)S(1)}, bf16[512,256]{1,0:T(8,128)(2,1)S(1)}, bf16[8,1024]{1,0:T(8,128)(2,1)S(1)}) custom-call(s32[1]{0:T(128)} %bitcast.c_ref, s32[1]{0:T(128)} %bitcast.1.x_ref, bf16[2,256,512]{2,1,0:T(8,128)(2,1)S(1)} %copy-done.4, ...), custom_call_target="tpu_custom_call" | custom-call | flops 1000000000 | bytes 1048576 | tf_op jit(solution)/shard_map/pallas_call | solution.py:279
  7.2 0.0 copy-start.8
  7.3 3.3 %collective-permute-start.2 = (bf16[16,512]{1,0:T(8,128)(2,1)S(1)}, bf16[16,512]{1,0:T(8,128)(2,1)S(1)}, u32[]{:S(2)}, u32[]{:S(2)}) collective-permute-start(bf16[16,512]{1,0:T(8,128)(2,1)S(1)} %get-tuple-element.33), channel_id=1, source_target_pairs={{0,8},{8,16},{16,24},{24,32},{32,40},{40,48},{48,56},{56,64},{64,7... | collective-permute-start | bytes 49160 | tf_op jit(solution)/shard_map/ppermute | solution.py:333
  10.6 0.7 slice_select_fusion.1
  11.3 0.1 collective-permute-done.2.halo_ref
  11.5 0.8 copy-done
  12.3 0.0 copy-done.5
  12.3 1.0 %shard_map.101 = (bf16[512,128]{1,0:T(8,128)(2,1)S(1)}, bf16[128,512]{1,0:T(8,128)(2,1)S(1)}, bf16[512,256]{1,0:T(8,128)(2,1)S(1)}, bf16[32,24,128]{2,1,0:T(8,128)(2,1)S(1)}) custom-call(bf16[512,512]{1,0:T(8,128)(2,1)S(1)} %get-tuple-element.37.tok_ref, bf16[16,512]{1,0:T(8,128)(2,1)S(1)} %collective-permute-done.2.halo_ref, ...), custom_call_target="tpu_custom_call" | custom-call | flops 1000000000 | bytes 1048576 | tf_op jit(solution)/shard_map/pallas_call | solution.py:279
  13.4 0.7 copy-done.18
  14.1 1.0 %collective-permute-done.3.rest_0_ = bf16[264,256]{1,0:T(8,128)(2,1)S(1)} collective-permute-done((bf16[264,256]{1,0:T(8,128)(2,1)S(1)}, bf16[264,256]{1,0:T(8,128)(2,1)S(1)}, u32[]{:S(2)}, u32[]{:S(2)}) %collective-permute-start.3) | collective-permute-done | bytes 135200 | tf_op jit(solution)/shard_map/ppermute | solution.py:292
  15.1 1.2 %collective-permute-start.6 = (bf16[264,256]{1,0:T(8,128)(2,1)S(1)}, bf16[264,256]{1,0:T(8,128)(2,1)S(1)}, u32[]{:S(2)}, u32[]{:S(2)}) collective-permute-start(bf16[264,256]{1,0:T(8,128)(2,1)S(1)} %collective-permute-done.3.rest_0_), channel_id=1, source_target_pairs={{0,4},{4,0},{1,5},{5,1},{2,6},{6,2},{3,7},{7,3},{8,12},{12,8},{9,1... | collective-permute-start | bytes 405512 | tf_op jit(solution)/shard_map/ppermute | solution.py:292
  16.3 0.1 collective-permute-start.7
  16.4 0.4 collective-permute-start.8
  16.8 0.7 fusion
  17.5 0.0 copy-start.24
  17.5 0.6 copy-done.24
  18.1 0.1 broadcast_in_dim.15
  18.2 0.1 broadcast_in_dim_reshape.3
  18.3 0.9 %copy-done.11 = bf16[512,256]{1,0:T(8,128)(2,1)S(1)} copy-done((bf16[512,256]{1,0:T(8,128)(2,1)S(1)}, bf16[512,256]{1,0:T(8,128)(2,1)}, u32[]{:S(2)}) %copy-start.11) | copy-done | bytes 262168
  19.3 0.9 %copy-done.15 = bf16[512,128]{1,0:T(8,128)(2,1)S(1)} copy-done((bf16[512,128]{1,0:T(8,128)(2,1)S(1)}, bf16[512,128]{1,0:T(8,128)(2,1)}, u32[]{:S(2)}) %copy-start.15) | copy-done | bytes 131096
  20.2 0.9 %copy-done.17 = bf16[128,512]{1,0:T(8,128)(2,1)S(1)} copy-done((bf16[128,512]{1,0:T(8,128)(2,1)S(1)}, bf16[128,512]{1,0:T(8,128)(2,1)}, u32[]{:S(2)}) %copy-start.17) | copy-done | bytes 131096
  21.1 2.6 %shard_map.102 = (bf16[512,768]{1,0:T(8,128)(2,1)S(1)}, bf16[32,24,128]{2,1,0:T(8,128)(2,1)}, bf16[512,256]{1,0:T(8,128)(2,1)S(1)}) custom-call(s32[1]{0:T(128)} %bitcast.c_ref, bf16[512,512]{1,0:T(8,128)(2,1)S(1)} %get-tuple-element.37.tok_ref, bf16[16,512]{1,0:T(8,128)(2,1)S(1)} %collective-permute-done.2.halo_ref, bf16[512,256]{1,0:T(8,128)(2,1)S(1)} %copy-done.11, ...), custom_call_target="tpu_custom_call" | custom-call | flops 1000000000 | bytes 1048576 | tf_op jit(solution)/shard_map/pallas_call | solution.py:279
  23.7 12.7 %all-to-all-start = ((bf16[32,24,128]{2,1,0:T(8,128)(2,1)}), bf16[32,24,128]{2,1,0:T(8,128)(2,1)S(1)}, u32[]{:S(2)}, u32[]{:S(2)}) async-start(bf16[32,24,128]{2,1,0:T(8,128)(2,1)} %get-tuple-element.52), calls=%async_computation | async-start | bytes 393216 | tf_op jit(solution)/shard_map/all_to_all | solution.py:363
  36.5 2.1 %collective-permute-start.11 = (bf16[520,256]{1,0:T(8,128)(2,1)S(1)}, bf16[520,256]{1,0:T(8,128)(2,1)S(1)}, u32[]{:S(2)}, u32[]{:S(2)}) collective-permute-start(bf16[520,256]{1,0:T(8,128)(2,1)S(1)} %pad_add_fusion), channel_id=1, source_target_pairs={{0,3},{1,0},{2,1},{3,2},{4,7},{5,4},{6,5},{7,6},{8,11},{9,8},{10,9... | collective-permute-start | bytes 798728 | tf_op jit(solution)/shard_map/ppermute | solution.py:292
  38.6 1.2 %collective-permute-start.10 = (bf16[520,256]{1,0:T(8,128)(2,1)S(1)}, bf16[520,256]{1,0:T(8,128)(2,1)S(1)}, u32[]{:S(2)}, u32[]{:S(2)}) collective-permute-start(bf16[520,256]{1,0:T(8,128)(2,1)S(1)} %pad_add_fusion), channel_id=1, source_target_pairs={{0,2},{1,3},{2,0},{3,1},{4,6},{5,7},{6,4},{7,5},{8,10},{9,11},{10,... | collective-permute-start | bytes 798728 | tf_op jit(solution)/shard_map/ppermute | solution.py:292
  39.9 4.4 %collective-permute-done.11.rest_2_ = bf16[520,256]{1,0:T(8,128)(2,1)S(1)} collective-permute-done((bf16[520,256]{1,0:T(8,128)(2,1)S(1)}, bf16[520,256]{1,0:T(8,128)(2,1)S(1)}, u32[]{:S(2)}, u32[]{:S(2)}) %collective-permute-start.11) | collective-permute-done | bytes 266272 | tf_op jit(solution)/shard_map/ppermute | solution.py:292
  44.3 6.7 %collective-permute-start.14 = (bf16[520,256]{1,0:T(8,128)(2,1)S(1)}, bf16[520,256]{1,0:T(8,128)(2,1)S(1)}, u32[]{:S(2)}, u32[]{:S(2)}) collective-permute-start(bf16[520,256]{1,0:T(8,128)(2,1)S(1)} %collective-permute-done.11.rest_2_), channel_id=1, source_target_pairs={{0,4},{4,0},{1,5},{5,1},{2,6},{6,2},{3,7},{7,3},{8,12},{12,8},{9,1... | collective-permute-start | bytes 798728 | tf_op jit(solution)/shard_map/ppermute | solution.py:292
  51.0 3.2 %collective-permute-done.9.rest_0_ = bf16[520,256]{1,0:T(8,128)(2,1)S(1)} collective-permute-done((bf16[520,256]{1,0:T(8,128)(2,1)S(1)}, bf16[520,256]{1,0:T(8,128)(2,1)S(1)}, u32[]{:S(2)}, u32[]{:S(2)}) %collective-permute-start.9) | collective-permute-done | bytes 266272 | tf_op jit(solution)/shard_map/ppermute | solution.py:292
  54.2 0.5 collective-permute-start.12
  54.6 0.8 shard_map.104
  55.4 9.2 %all-to-all-start.1 = ((bf16[32,16,128]{2,1,0:T(8,128)(2,1)}), bf16[32,16,128]{2,1,0:T(8,128)(2,1)S(1)}, u32[]{:S(2)}, u32[]{:S(2)}) async-start(bf16[32,16,128]{2,1,0:T(8,128)(2,1)} %shard_map.104), calls=%async_computation.1 | async-start | bytes 262144 | tf_op jit(solution)/shard_map/all_to_all | solution.py:367
  64.6 0.9 %copy-done.19 = bf16[512,256]{1,0:T(8,128)(2,1)S(1)} copy-done((bf16[512,256]{1,0:T(8,128)(2,1)S(1)}, bf16[512,256]{1,0:T(8,128)(2,1)}, u32[]{:S(2)}) %copy-start.19) | copy-done | bytes 262168
  65.6 5.9 %shard_map.103.y_ref = bf16[512,1024]{1,0:T(8,128)(2,1)S(1)} custom-call(bf16[512,256]{1,0:T(8,128)(2,1)S(1)} %copy-done.19, bf16[512,768]{1,0:T(8,128)(2,1)S(1)} %get-tuple-element.46.xa1_ref, bf16[512,256]{1,0:T(8,128)(2,1)S(1)} %get-tuple-element.47.seen_ref, bf16[8,256]{1,0:T(8,128)(2,1)S(1)} %pad_add_fusion.2.p0_ref, ...), custom_call_target="tpu_custom_call" | custom-call | flops 2000000000 | bytes 1048576 | tf_op jit(solution)/shard_map/pallas_call | solution.py:279
  71.5 1.0 %copy-done.12 = bf16[512,1024]{1,0:T(8,128)(2,1)} copy-done((bf16[512,1024]{1,0:T(8,128)(2,1)}, bf16[512,1024]{1,0:T(8,128)(2,1)S(1)}, u32[]{:S(2)}) %copy-start.12) | copy-done | bytes 1048600
  72.5 2.0 %all-to-all-done.1.back_ref = bf16[32,16,128]{2,1,0:T(8,128)(2,1)S(1)} async-done(((bf16[32,16,128]{2,1,0:T(8,128)(2,1)}), bf16[32,16,128]{2,1,0:T(8,128)(2,1)S(1)}, u32[]{:S(2)}, u32[]{:S(2)}) %all-to-all-start.1) | async-done | bytes 131104 | tf_op jit(solution)/shard_map/all_to_all | solution.py:367
  74.6 1.0 %copy-done.9 = bf16[512,512]{1,0:T(8,128)(2,1)S(1)} copy-done((bf16[512,512]{1,0:T(8,128)(2,1)S(1)}, bf16[512,512]{1,0:T(8,128)(2,1)}, u32[]{:S(2)}) %copy-start.9) | copy-done | bytes 524312
  75.6 1.2 %copy-done.13 = bf16[512,1024]{1,0:T(8,128)(2,1)S(1)} copy-done((bf16[512,1024]{1,0:T(8,128)(2,1)S(1)}, bf16[512,1024]{1,0:T(8,128)(2,1)}, u32[]{:S(2)}) %copy-start.13) | copy-done | bytes 1048600
  76.8 1.4 %shard_map.105 = (bf16[512,1024]{1,0:T(8,128)(2,1)S(1)}, bf16[512,1024]{1,0:T(8,128)(2,1)S(1)}, bf16[1024,512]{1,0:T(8,128)(2,1)S(1)}, bf16[8,1024]{1,0:T(8,128)(2,1)S(1)}) custom-call(s32[1]{0:T(128)} %bitcast.c_ref, bf16[512,512]{1,0:T(8,128)(2,1)S(1)} %copy-done.9, bf16[512,256]{1,0:T(8,128)(2,1)S(1)} %get-tuple-element.47.seen_ref, ...), custom_call_target="tpu_custom_call" | custom-call | flops 2000000000 | bytes 1048576 | tf_op jit(solution)/shard_map/pallas_call | solution.py:279
  78.2 1.4 %shard_map.107 = bf16[256,512]{1,0:T(8,128)(2,1)S(1)} custom-call(s32[1]{0:T(128)} %bitcast.c_ref, bf16[32,16,128]{2,1,0:T(8,128)(2,1)S(1)} %all-to-all-done.1.back_ref, bf16[512,256]{1,0:T(8,128)(2,1)S(1)} %get-tuple-element.47.seen_ref, bf16[512,1024]{1,0:T(8,128)(2,1)S(1)} %get-tuple-element.55.yg_ref, bf16[512,1024]{1,0:T(8,128)(2,1)S(1)} %get-tuple-element.56.eg_ref, ...), custom_call_target="tpu_custom_call" | custom-call | flops 1000000000 | bytes 1048576 | tf_op jit(solution)/shard_map/pallas_call | solution.py:279
  79.6 1.5 %collective-permute-start.15 = (bf16[256,512]{1,0:T(8,128)(2,1)S(1)}, bf16[256,512]{1,0:T(8,128)(2,1)S(1)}, u32[]{:S(2)}, u32[]{:S(2)}) collective-permute-start(bf16[256,512]{1,0:T(8,128)(2,1)S(1)} %shard_map.107), channel_id=1, source_target_pairs={{0,4},{4,0},{1,5},{5,1},{2,6},{6,2},{3,7},{7,3},{8,12},{12,8},{9,1... | collective-permute-start | bytes 786440 | tf_op jit(solution)/shard_map/ppermute | solution.py:292
  81.1 1.4 %shard_map.106.own_ref = bf16[256,512]{1,0:T(8,128)(2,1)S(1)} custom-call(s32[1]{0:T(128)} %bitcast.c_ref, bf16[32,16,128]{2,1,0:T(8,128)(2,1)S(1)} %all-to-all-done.1.back_ref, bf16[512,256]{1,0:T(8,128)(2,1)S(1)} %get-tuple-element.47.seen_ref, bf16[512,1024]{1,0:T(8,128)(2,1)S(1)} %get-tuple-element.55.yg_ref, ...), custom_call_target="tpu_custom_call" | custom-call | flops 1000000000 | bytes 1048576 | tf_op jit(solution)/shard_map/pallas_call | solution.py:279
  82.5 0.8 shard_map.108
  (57 shorter events, 0.2 us)
Async XLA Ops:
  0.0 6.3 %collective-permute-start = (bf16[2,256,512]{2,1,0:T(8,128)(2,1)}, bf16[2,256,512]{2,1,0:T(8,128)(2,1)S(1)}, u32[]{:S(2)}, u32[]{:S(2)}) collective-permute-start(bf16[2,256,512]{2,1,0:T(8,128)(2,1)} %tokens_ref.1), channel_id=1, source_target_pairs={{0,4},{4,0},{1,5},{5,1},{2,6},{6,2},{3,7},{7,3},{8,12},{12,8},{9,1... | collective-permute-start | bytes 1572872 | tf_op jit(solution)/shard_map/ppermute | solution.py:292
  3.2 3.1 %collective-permute-start.1 = (bf16[2,16,256]{2,1,0:T(8,128)(2,1)}, bf16[2,16,256]{2,1,0:T(8,128)(2,1)S(1)}, u32[]{:S(2)}, u32[]{:S(2)}) collective-permute-start(bf16[2,16,256]{2,1,0:T(8,128)(2,1)} %bitcast.3), channel_id=1, source_target_pairs={{0,4},{4,0},{1,5},{5,1},{2,6},{6,2},{3,7},{7,3},{8,12},{12,8},{9,1... | collective-permute-start | bytes 49160 | tf_op jit(solution)/shard_map/ppermute | solution.py:292
  3.2 1.1 %copy-start.3 = (bf16[4,256]{1,0:T(4,128)(2,1)S(1)}, bf16[4,256]{1,0:T(4,128)(2,1)}, u32[]{:S(2)}) copy-start(bf16[4,256]{1,0:T(4,128)(2,1)} %cx_ref.1) | copy-start | bytes 6148
  3.2 3.1 %copy-start.4 = (bf16[2,256,512]{2,1,0:T(8,128)(2,1)S(1)}, bf16[2,256,512]{2,1,0:T(8,128)(2,1)}, u32[]{:S(2)}) copy-start(bf16[2,256,512]{2,1,0:T(8,128)(2,1)} %tokens_ref.1) | copy-start | bytes 1572868
  4.3 2.0 %copy-start.6 = (bf16[2,256,16]{1,2,0:T(8,128)(2,1)S(1)}, bf16[2,256,16]{1,2,0:T(8,128)(2,1)}, u32[]{:S(2)}) copy-start(bf16[2,256,16]{1,2,0:T(8,128)(2,1)} %param.11) | copy-start | bytes 49156
  4.3 9.8 %collective-permute-start.5 = (bf16[264,256]{1,0:T(8,128)(2,1)S(1)}, bf16[264,256]{1,0:T(8,128)(2,1)S(1)}, u32[]{:S(2)}, u32[]{:S(2)}) collective-permute-start(bf16[264,256]{1,0:T(8,128)(2,1)S(1)} %pad_add_fusion.1), channel_id=1, source_target_pairs={{0,3},{1,0},{2,1},{3,2},{4,7},{5,4},{6,5},{7,6},{8,11},{9,8},{10,9... | collective-permute-start | bytes 405512 | tf_op jit(solution)/shard_map/ppermute | solution.py:292
  5.1 8.9 %collective-permute-start.4 = (bf16[264,256]{1,0:T(8,128)(2,1)S(1)}, bf16[264,256]{1,0:T(8,128)(2,1)S(1)}, u32[]{:S(2)}, u32[]{:S(2)}) collective-permute-start(bf16[264,256]{1,0:T(8,128)(2,1)S(1)} %pad_add_fusion.1), channel_id=1, source_target_pairs={{0,2},{1,3},{2,0},{3,1},{4,6},{5,7},{6,4},{7,5},{8,10},{9,11},{10,... | collective-permute-start | bytes 405512 | tf_op jit(solution)/shard_map/ppermute | solution.py:292
  5.7 9.4 %collective-permute-start.3 = (bf16[264,256]{1,0:T(8,128)(2,1)S(1)}, bf16[264,256]{1,0:T(8,128)(2,1)S(1)}, u32[]{:S(2)}, u32[]{:S(2)}) collective-permute-start(bf16[264,256]{1,0:T(8,128)(2,1)S(1)} %pad_add_fusion.1), channel_id=1, source_target_pairs={{0,1},{1,2},{2,3},{3,0},{4,5},{5,6},{6,7},{7,4},{8,9},{9,10},{10,1... | collective-permute-start | bytes 405512 | tf_op jit(solution)/shard_map/ppermute | solution.py:292
  6.3 4.3 %copy-start.2 = (bf16[512,256]{1,0:T(8,128)(2,1)S(1)}, bf16[512,256]{1,0:T(8,128)(2,1)}, u32[]{:S(2)}) copy-start(bf16[512,256]{1,0:T(8,128)(2,1)} %wz0_ref) | copy-start | bytes 786436
  7.2 4.2 %copy-start.10 = (bf16[512,256]{1,0:T(8,128)(2,1)}, bf16[512,256]{1,0:T(8,128)(2,1)S(1)}, u32[]{:S(2)}) copy-start(bf16[512,256]{1,0:T(8,128)(2,1)S(1)} %get-tuple-element.34.tail_ref) | copy-start | bytes 786436
  7.2 11.1 %copy-start.8 = (bf16[512,512]{1,0:T(8,128)(2,1)}, bf16[512,512]{1,0:T(8,128)(2,1)S(1)}, u32[]{:S(2)}) copy-start(bf16[512,512]{1,0:T(8,128)(2,1)S(1)} %get-tuple-element.37.tok_ref) | copy-start | bytes 1572868
  7.3 4.0 %copy-start.1 = (bf16[256,512]{1,0:T(8,128)(2,1)S(1)}, bf16[256,512]{1,0:T(8,128)(2,1)}, u32[]{:S(2)}) copy-start(bf16[256,512]{1,0:T(8,128)(2,1)} %wo0_ref) | copy-start | bytes 786436
  7.3 4.2 %collective-permute-start.2 = (bf16[16,512]{1,0:T(8,128)(2,1)S(1)}, bf16[16,512]{1,0:T(8,128)(2,1)S(1)}, u32[]{:S(2)}, u32[]{:S(2)}) collective-permute-start(bf16[16,512]{1,0:T(8,128)(2,1)S(1)} %get-tuple-element.33), channel_id=1, source_target_pairs={{0,8},{8,16},{16,24},{24,32},{32,40},{40,48},{48,56},{56,64},{64,7... | collective-permute-start | bytes 49160 | tf_op jit(solution)/shard_map/ppermute | solution.py:333
  11.3 1.0 %copy-start = (bf16[512,256]{1,0:T(8,128)(2,1)S(1)}, bf16[512,256]{1,0:T(8,128)(2,1)}, u32[]{:S(2)}) copy-start(bf16[512,256]{1,0:T(8,128)(2,1)} %w_ref.1) | copy-start | bytes 786436
  11.3 1.0 %copy-start.5 = (bf16[512,128]{1,0:T(8,128)(2,1)S(1)}, bf16[512,128]{1,0:T(8,128)(2,1)}, u32[]{:S(2)}) copy-start(bf16[512,128]{1,0:T(8,128)(2,1)} %wbc_ref.1) | copy-start | bytes 393220
  11.5 0.8 copy-start.7
  13.3 0.7 copy-start.18
  14.0 3.4 %copy-start.14 = (bf16[512,128]{1,0:T(8,128)(2,1)}, bf16[512,128]{1,0:T(8,128)(2,1)S(1)}, u32[]{:S(2)}) copy-start(bf16[512,128]{1,0:T(8,128)(2,1)S(1)} %get-tuple-element.39.bc_ref) | copy-start | bytes 393220
  14.0 3.4 %copy-start.16 = (bf16[128,512]{1,0:T(8,128)(2,1)}, bf16[128,512]{1,0:T(8,128)(2,1)S(1)}, u32[]{:S(2)}) copy-start(bf16[128,512]{1,0:T(8,128)(2,1)S(1)} %get-tuple-element.38.bt_ref) | copy-start | bytes 393220
  15.1 2.4 %copy-start.23 = (bf16[256]{0:T(256)(128)(2,1)S(1)}, bf16[256]{0:T(256)(128)(2,1)}, u32[]{:S(2)}) copy-start(bf16[256]{0:T(256)(128)(2,1)} %param.18) | copy-start | bytes 1540
  15.1 3.2 %collective-permute-start.6 = (bf16[264,256]{1,0:T(8,128)(2,1)S(1)}, bf16[264,256]{1,0:T(8,128)(2,1)S(1)}, u32[]{:S(2)}, u32[]{:S(2)}) collective-permute-start(bf16[264,256]{1,0:T(8,128)(2,1)S(1)} %collective-permute-done.3.rest_0_), channel_id=1, source_target_pairs={{0,4},{4,0},{1,5},{5,1},{2,6},{6,2},{3,7},{7,3},{8,12},{12,8},{9,1... | collective-permute-start | bytes 405512 | tf_op jit(solution)/shard_map/ppermute | solution.py:292
  16.3 2.0 %collective-permute-start.7 = (bf16[264,256]{1,0:T(8,128)(2,1)S(1)}, bf16[264,256]{1,0:T(8,128)(2,1)S(1)}, u32[]{:S(2)}, u32[]{:S(2)}) collective-permute-start(bf16[264,256]{1,0:T(8,128)(2,1)S(1)} %collective-permute-done.4.rest_1_), channel_id=1, source_target_pairs={{0,4},{4,0},{1,5},{5,1},{2,6},{6,2},{3,7},{7,3},{8,12},{12,8},{9,1... | collective-permute-start | bytes 405512 | tf_op jit(solution)/shard_map/ppermute | solution.py:292
  16.4 1.9 %collective-permute-start.8 = (bf16[264,256]{1,0:T(8,128)(2,1)S(1)}, bf16[264,256]{1,0:T(8,128)(2,1)S(1)}, u32[]{:S(2)}, u32[]{:S(2)}) collective-permute-start(bf16[264,256]{1,0:T(8,128)(2,1)S(1)} %collective-permute-done.5.rest_2_), channel_id=1, source_target_pairs={{0,4},{4,0},{1,5},{5,1},{2,6},{6,2},{3,7},{7,3},{8,12},{12,8},{9,1... | collective-permute-start | bytes 405512 | tf_op jit(solution)/shard_map/ppermute | solution.py:292
  17.5 0.7 copy-start.24
  18.3 1.0 %copy-start.11 = (bf16[512,256]{1,0:T(8,128)(2,1)S(1)}, bf16[512,256]{1,0:T(8,128)(2,1)}, u32[]{:S(2)}) copy-start(bf16[512,256]{1,0:T(8,128)(2,1)} %copy-done.10) | copy-start | bytes 786436
  19.3 0.9 %copy-start.15 = (bf16[512,128]{1,0:T(8,128)(2,1)S(1)}, bf16[512,128]{1,0:T(8,128)(2,1)}, u32[]{:S(2)}) copy-start(bf16[512,128]{1,0:T(8,128)(2,1)} %copy-done.14) | copy-start | bytes 393220
  20.2 0.9 %copy-start.17 = (bf16[128,512]{1,0:T(8,128)(2,1)S(1)}, bf16[128,512]{1,0:T(8,128)(2,1)}, u32[]{:S(2)}) copy-start(bf16[128,512]{1,0:T(8,128)(2,1)} %copy-done.16) | copy-start | bytes 393220
  23.7 12.7 %copy-start.20 = (bf16[256,256]{1,0:T(8,128)(2,1)S(1)}, bf16[256,256]{1,0:T(8,128)(2,1)}, u32[]{:S(2)}) copy-start(bf16[256,256]{1,0:T(8,128)(2,1)} %slice_select_fusion.1) | copy-start | bytes 393220
  23.7 12.7 %copy-start.21 = (bf16[128,256]{1,0:T(8,128)(2,1)S(1)}, bf16[128,256]{1,0:T(8,128)(2,1)}, u32[]{:S(2)}) copy-start(bf16[128,256]{1,0:T(8,128)(2,1)} %get-tuple-element.59) | copy-start | bytes 196612
  23.7 12.7 %copy-start.22 = (bf16[128,256]{1,0:T(8,128)(2,1)S(1)}, bf16[128,256]{1,0:T(8,128)(2,1)}, u32[]{:S(2)}) copy-start(bf16[128,256]{1,0:T(8,128)(2,1)} %get-tuple-element.60) | copy-start | bytes 196612
  23.7 30.9 %all-to-all-start = ((bf16[32,24,128]{2,1,0:T(8,128)(2,1)}), bf16[32,24,128]{2,1,0:T(8,128)(2,1)S(1)}, u32[]{:S(2)}, u32[]{:S(2)}) async-start(bf16[32,24,128]{2,1,0:T(8,128)(2,1)} %get-tuple-element.52), calls=%async_computation | async-start | bytes 393216 | tf_op jit(solution)/shard_map/all_to_all | solution.py:363
  36.5 7.8 %collective-permute-start.11 = (bf16[520,256]{1,0:T(8,128)(2,1)S(1)}, bf16[520,256]{1,0:T(8,128)(2,1)S(1)}, u32[]{:S(2)}, u32[]{:S(2)}) collective-permute-start(bf16[520,256]{1,0:T(8,128)(2,1)S(1)} %pad_add_fusion), channel_id=1, source_target_pairs={{0,3},{1,0},{2,1},{3,2},{4,7},{5,4},{6,5},{7,6},{8,11},{9,8},{10,9... | collective-permute-start | bytes 798728 | tf_op jit(solution)/shard_map/ppermute | solution.py:292
  38.6 12.3 %collective-permute-start.10 = (bf16[520,256]{1,0:T(8,128)(2,1)S(1)}, bf16[520,256]{1,0:T(8,128)(2,1)S(1)}, u32[]{:S(2)}, u32[]{:S(2)}) collective-permute-start(bf16[520,256]{1,0:T(8,128)(2,1)S(1)} %pad_add_fusion), channel_id=1, source_target_pairs={{0,2},{1,3},{2,0},{3,1},{4,6},{5,7},{6,4},{7,5},{8,10},{9,11},{10,... | collective-permute-start | bytes 798728 | tf_op jit(solution)/shard_map/ppermute | solution.py:292
  39.9 14.3 %collective-permute-start.9 = (bf16[520,256]{1,0:T(8,128)(2,1)S(1)}, bf16[520,256]{1,0:T(8,128)(2,1)S(1)}, u32[]{:S(2)}, u32[]{:S(2)}) collective-permute-start(bf16[520,256]{1,0:T(8,128)(2,1)S(1)} %pad_add_fusion), channel_id=1, source_target_pairs={{0,1},{1,2},{2,3},{3,0},{4,5},{5,6},{6,7},{7,4},{8,9},{9,10},{10,1... | collective-permute-start | bytes 798728 | tf_op jit(solution)/shard_map/ppermute | solution.py:292
  44.3 30.3 %collective-permute-start.14 = (bf16[520,256]{1,0:T(8,128)(2,1)S(1)}, bf16[520,256]{1,0:T(8,128)(2,1)S(1)}, u32[]{:S(2)}, u32[]{:S(2)}) collective-permute-start(bf16[520,256]{1,0:T(8,128)(2,1)S(1)} %collective-permute-done.11.rest_2_), channel_id=1, source_target_pairs={{0,4},{4,0},{1,5},{5,1},{2,6},{6,2},{3,7},{7,3},{8,12},{12,8},{9,1... | collective-permute-start | bytes 798728 | tf_op jit(solution)/shard_map/ppermute | solution.py:292
  51.0 23.6 %collective-permute-start.13 = (bf16[520,256]{1,0:T(8,128)(2,1)S(1)}, bf16[520,256]{1,0:T(8,128)(2,1)S(1)}, u32[]{:S(2)}, u32[]{:S(2)}) collective-permute-start(bf16[520,256]{1,0:T(8,128)(2,1)S(1)} %collective-permute-done.10.rest_1_), channel_id=1, source_target_pairs={{0,4},{4,0},{1,5},{5,1},{2,6},{6,2},{3,7},{7,3},{8,12},{12,8},{9,1... | collective-permute-start | bytes 798728 | tf_op jit(solution)/shard_map/ppermute | solution.py:292
  54.2 20.4 %collective-permute-start.12 = (bf16[520,256]{1,0:T(8,128)(2,1)S(1)}, bf16[520,256]{1,0:T(8,128)(2,1)S(1)}, u32[]{:S(2)}, u32[]{:S(2)}) collective-permute-start(bf16[520,256]{1,0:T(8,128)(2,1)S(1)} %collective-permute-done.9.rest_0_), channel_id=1, source_target_pairs={{0,4},{4,0},{1,5},{5,1},{2,6},{6,2},{3,7},{7,3},{8,12},{12,8},{9,1... | collective-permute-start | bytes 798728 | tf_op jit(solution)/shard_map/ppermute | solution.py:292
  55.4 19.1 %all-to-all-start.1 = ((bf16[32,16,128]{2,1,0:T(8,128)(2,1)}), bf16[32,16,128]{2,1,0:T(8,128)(2,1)S(1)}, u32[]{:S(2)}, u32[]{:S(2)}) async-start(bf16[32,16,128]{2,1,0:T(8,128)(2,1)} %shard_map.104), calls=%async_computation.1 | async-start | bytes 262144 | tf_op jit(solution)/shard_map/all_to_all | solution.py:367
  64.6 1.0 %copy-start.19 = (bf16[512,256]{1,0:T(8,128)(2,1)S(1)}, bf16[512,256]{1,0:T(8,128)(2,1)}, u32[]{:S(2)}) copy-start(bf16[512,256]{1,0:T(8,128)(2,1)} %copy-done.18) | copy-start | bytes 786436
  71.5 1.0 %copy-start.12 = (bf16[512,1024]{1,0:T(8,128)(2,1)}, bf16[512,1024]{1,0:T(8,128)(2,1)S(1)}, u32[]{:S(2)}) copy-start(bf16[512,1024]{1,0:T(8,128)(2,1)S(1)} %shard_map.103.y_ref) | copy-start | bytes 3145732
  74.6 1.0 %copy-start.9 = (bf16[512,512]{1,0:T(8,128)(2,1)S(1)}, bf16[512,512]{1,0:T(8,128)(2,1)}, u32[]{:S(2)}) copy-start(bf16[512,512]{1,0:T(8,128)(2,1)} %copy-done.8) | copy-start | bytes 1572868
  75.6 1.2 %copy-start.13 = (bf16[512,1024]{1,0:T(8,128)(2,1)S(1)}, bf16[512,1024]{1,0:T(8,128)(2,1)}, u32[]{:S(2)}) copy-start(bf16[512,1024]{1,0:T(8,128)(2,1)} %copy-done.12) | copy-start | bytes 3145732
  79.6 2.9 %collective-permute-start.15 = (bf16[256,512]{1,0:T(8,128)(2,1)S(1)}, bf16[256,512]{1,0:T(8,128)(2,1)S(1)}, u32[]{:S(2)}, u32[]{:S(2)}) collective-permute-start(bf16[256,512]{1,0:T(8,128)(2,1)S(1)} %shard_map.107), channel_id=1, source_target_pairs={{0,4},{4,0},{1,5},{5,1},{2,6},{6,2},{3,7},{7,3},{8,12},{12,8},{9,1... | collective-permute-start | bytes 786440 | tf_op jit(solution)/shard_map/ppermute | solution.py:292
where the time goes:
time: 83.9 us; the launch traced here: 83.4 us
  starting transfers between devices  44.3 us (53%)
  Pallas kernels  16.2 us (19%)
  waiting for transfers between devices  10.8 us (13%)
  local copies, waits for them, and re-layouts  9.98 us (12%)
  other arithmetic  1.77 us (2%)
    ppermute x15, starting transfers between devices, around(): lax.ppermute(value, axis, [(k, (k + steps) % count) for k in range(count)])  19 us
    pallas_call x9, Pallas kernels, call(): pl.pallas_call(kernel, out_shape=[jax.ShapeDtypeStruct(shape, dtype) for...  16.2 us
    all_to_all x1, starting transfers between devices, layer(): arrived = lax.all_to_all(msg, CHIPS, 0, 0)  12.7 us
    all_to_all x1, starting transfers between devices, layer(): back = lax.all_to_all(carries, CHIPS, 0, 0)  9.21 us
    unnamed x50, local copies, waits for them, and re-layouts  9.16 us
    ppermute x15, waiting for transfers between devices, around(): lax.ppermute(value, axis, [(k, (k + steps) % count) for k in range(count)])  8.58 us
    ppermute x1, starting transfers between devices, layer(): halo = lax.ppermute(edge, CHIPS, [(k, k + 1) for k in range(chips - 1)])  3.33 us
    all_to_all x1, waiting for transfers between devices, layer(): back = lax.all_to_all(carries, CHIPS, 0, 0)  2.03 us
  transfers between devices with their start and end apart: 18, of which 5 were waited for; matrix products, arithmetic and copies ran while one was open for 3% of the time, Pallas kernels for 12%

commit v1 on v0

--- a/solution.py
+++ b/solution.py
@@ -123,18 +123,20 @@
     shard_states(w_ref[...], cx_ref[...].astype(F32), 0, 0, tok_ref, halo_ref, tail_ref, bt_ref, xa_ref, msg_ref)
 
 
-def others_kernel(c_ref, tok_ref, halo_ref, tail_ref, bt_ref, bc_ref, logp_ref, own_msg_ref, *rest):
+def others_kernel(c_ref, tok_ref, halo_ref, tail_ref, bt_ref, bc_ref, logp_ref, own_msg_ref, own_prm_ref, *rest):
     here, there = rest[0 : SHARDS - 1], rest[SHARDS - 1 : 2 * SHARDS - 2]
-    xa_ref, msg_ref, seen_ref, w_ref = rest[2 * SHARDS - 2 :]
+    xa_ref, msg_ref, seen_ref, prm_ref, w_ref = rest[2 * SHARDS - 2 :]
     core = c_ref[0]
     seen_ref[:, 0:LANES] = bc_ref[...]
     seen_ref[:, LANES:] = logp_ref[...]
     half, wide = w_ref.shape[0] // 2, w_ref.shape[1]
     msg_ref[...] = own_msg_ref[...]
+    prm_ref[:, 0:wide] = own_prm_ref[...]
     for r in range(1, SHARDS):
         a, b = here[r - 1][0:half], there[r - 1][0:half]
         w_ref[0:half] = jnp.where(core == 0, a, b)
         w_ref[half : 2 * half] = jnp.where(core == 0, b, a)
+        prm_ref[:, r * wide : (r + 1) * wide] = here[r - 1][half : half + 8]
         taps = here[r - 1][half : half + 8].astype(F32)
         shard_states(w_ref[...], taps, r, (r - 1) * wide, tok_ref, halo_ref, tail_ref, bt_ref, xa_ref, msg_ref)
 
@@ -148,10 +150,8 @@
     lax.fori_loop(0, s_ref.shape[0], step, jnp.zeros((PART, LANES), F32), unroll=8)
 
 
-def intra_kernel(xa0_ref, xa1_ref, seen_ref, p0_ref, *rest):
-    z_refs, y_ref = rest[:-1], rest[-1]
+def intra_kernel(xa0_ref, xa1_ref, seen_ref, prm_ref, y_ref):
     length, wide = xa0_ref.shape
-    depth = z_refs[0].shape[0] - 8
     blocks = length // BLOCK
     lower_block = lower_ones(BLOCK)
     keep = iota((BLOCK, BLOCK), 0) >= iota((BLOCK, BLOCK), 1)
@@ -173,9 +173,7 @@
     for j in range(SHARDS * wide // LANES):
         lanes = slice(j * LANES, (j + 1) * LANES)
         to_lanes = spread(j * LANES, LANES)
-        r, at = divmod(j * LANES, wide)
-        extra = p0_ref[...] if r == 0 else z_refs[r - 1][depth : depth + 8]
-        skip = extra[1:2, at : at + LANES].astype(F32)
+        skip = prm_ref[CONV + 1 : CONV + 2, lanes].astype(F32)
         state = None
         for b in range(blocks):
             if j * LANES < wide:
@@ -200,9 +198,9 @@
             y_ref[span[b], lanes] = y.astype(BF16)
 
 
-def gate_kernel(c_ref, tok_ref, seen_ref, y_ref, wz0_ref, wo0_ref, p0_ref, *rest):
+def gate_kernel(c_ref, tok_ref, seen_ref, y_ref, wz0_ref, wo0_ref, *rest):
     here, there = rest[0 : SHARDS - 1], rest[SHARDS - 1 : 2 * SHARDS - 2]
-    yg_ref, eg_ref, wo_ref, gain_ref, wz_ref = rest[2 * SHARDS - 2 :]
+    yg_ref, eg_ref, wo_ref, wz_ref = rest[2 * SHARDS - 2 :]
     core = c_ref[0]
     depth, wide = wz0_ref.shape
     half, q = depth // 2, wide // 2
@@ -212,7 +210,6 @@
     for r in range(SHARDS):
         if r == 0:
             wz_ref[...] = wz0_ref[...]
-            extra = p0_ref[...]
         else:
             a, b = here[r - 1], there[r - 1]
             wz_ref[0:half] = jnp.where(core == 0, a[0:half], b[0:half])
@@ -222,9 +219,7 @@
                 lanes = slice(s * wide, (s + 1) * wide)
                 wo_ref[r * wide : r * wide + q, lanes] = jnp.where(core == 0, a[part], b[part])
                 wo_ref[r * wide + q : (r + 1) * wide, lanes] = jnp.where(core == 0, b[part], a[part])
-            extra = a[2 * half : 2 * half + 8]
         lanes = slice(r * wide, (r + 1) * wide)
-        gain_ref[:, lanes] = extra
         gate = silu(dot(tok_ref[...], wz_ref[...]).astype(BF16).astype(F32))
         yg_ref[:, lanes] = (y_ref[:, lanes].astype(F32) * gate).astype(BF16)
         eg_ref[:, lanes] = (dot(grow, spread(r * wide, wide)) * gate).astype(BF16)
@@ -242,7 +237,7 @@
         carry = jnp.concatenate([back_ref[j * parts + q] for q in range(parts)], axis=0)
         v = yg_ref[rows, lanes].astype(F32) + eg_ref[rows, lanes].astype(F32) * dot(read, carry)
         mean = dot(hi_lo(v * v), same_head) * (1.0 / 64.0)
-        gain = gain_ref[0:1, lanes].astype(F32)
+        gain = gain_ref[CONV : CONV + 1, lanes].astype(F32)
         normed_ref[:, lanes] = (v * lax.rsqrt(mean + 1e-05) * gain).astype(BF16)
     return dot(normed_ref[...], wo_ref[...]).astype(BF16)
 
@@ -312,12 +307,15 @@
     parts = width // LANES * (STATE // PART)
 
     low = core == 0
-    first = padded(jnp.where(low, w_x[:half], w_x[half:]), 0, half + 8) + padded(conv_x, half, half + 8)
+    extra = (
+        padded(conv_x, 0, 8) + padded(gain[None], CONV, 8) + padded(jnp.repeat(skip, wide // skip.shape[0])[None], CONV + 1, 8)
+    )
+    first = padded(jnp.where(low, w_x[:half], w_x[half:]), 0, half + 8) + padded(extra, half, half + 8)
     x_here = [around(first, "mix", r) for r in (2, 1, 3)]
     x_here = [x_here[1], x_here[0], x_here[2]]
     got = around(tokens, "seq_2", 1)
     got_log = around(logs, "seq_2", 1)
-    tok, edge, logp, tail, extra = call(
+    tok, edge, logp, tail, totals = call(
         decay_kernel,
         [
             ((both, depth), BF16),
@@ -334,47 +332,44 @@
     bc, bt, xa0, own_msg = call(
         own_kernel,
         [((both, 2 * STATE), BF16), ((2 * STATE, both), BF16), ((both, wide), BF16), ((parts, PART + 8, LANES), BF16)],
-        (tok, halo, tail, extra, w_bc, conv_bc, w_x, conv_x),
+        (tok, halo, tail, totals, w_bc, conv_bc, w_x, conv_x),
         [VMEM] * 4 + [ANY] * 4,
         flops=10**9,
     )
-    w_z, w_out, gain, skip, tok = lax.optimization_barrier((w_z, w_out, gain, skip, tok))
-    p0 = padded(gain[None], 0, 8) + padded(jnp.repeat(skip, wide // skip.shape[0])[None], 1, 8)
-    out_half = jnp.where(low, w_out[: wide // 2], w_out[wide // 2 :])
-    rows = 2 * half + 8
-    second = (
-        padded(jnp.where(low, w_z[:half], w_z[half:]), 0, rows)
-        + padded(out_half[:, :wide], half, rows)
-        + padded(out_half[:, wide:], half + wide // 2, rows)
-        + padded(p0, 2 * half, rows)
-    )
-    z_here = [around(second, "mix", r) for r in range(1, SHARDS)]
-
-    (x_here, own_msg) = lax.optimization_barrier((x_here, own_msg))
     x_there = [around(part, "seq_2", 1) for part in x_here]
-    xa1, msg, seen = call(
+    xa1, msg, seen, prm = call(
         others_kernel,
-        [((both, width - wide), BF16), ((parts, PART + 8, LANES), BF16), ((both, 2 * LANES), BF16)],
-        (core_s, tok, halo, tail, bt, bc, logp, own_msg, *x_here, *x_there),
-        [SMEM] + [VMEM] * 13,
+        [((both, width - wide), BF16), ((parts, PART + 8, LANES), BF16), ((both, 2 * LANES), BF16), ((8, width), BF16)],
+        (core_s, tok, halo, tail, bt, bc, logp, own_msg, extra, *x_here, *x_there),
+        [SMEM] + [VMEM] * 14,
         scratch=[pltpu.VMEM((depth, wide), BF16)],
         flops=10**9,
     )
     arrived = lax.all_to_all(msg, CHIPS, 0, 0)
-    (y,) = call(intra_kernel, [((both, width), BF16)], (xa0, xa1, seen, p0, *z_here), [VMEM] * 7, flops=2 * 10**9)
+    w_z, w_out, _ = lax.optimization_barrier((w_z, w_out, msg))
+    out_half = jnp.where(low, w_out[: wide // 2], w_out[wide // 2 :])
+    second = (
+        padded(jnp.where(low, w_z[:half], w_z[half:]), 0, depth)
+        + padded(out_half[:, :wide], half, depth)
+        + padded(out_half[:, wide:], half + wide // 2, depth)
+    )
+    z_here = [around(second, "mix", r) for r in (2, 1, 3)]
+    z_here = [z_here[1], z_here[0], z_here[2]]
     (carries,) = call(scan_kernel, [((parts, PART, LANES), BF16)], (arrived,), [VMEM], flops=10**7)
+    back = lax.all_to_all(carries, CHIPS, 0, 0)
+    (y,) = call(intra_kernel, [((both, width), BF16)], (xa0, xa1, seen, prm), [VMEM] * 4, flops=2 * 10**9)
+    z_here, y = lax.optimization_barrier((z_here, y))
     z_there = [around(part, "seq_2", 1) for part in z_here]
-    back = lax.all_to_all(carries, CHIPS, 0, 0)
     y, back = lax.optimization_barrier((y, back))
-    yg, eg, wo, gains = call(
+    yg, eg, wo = call(
         gate_kernel,
-        [((both, width), BF16), ((both, width), BF16), ((width, depth), BF16), ((8, width), BF16)],
-        (core_s, tok, seen, y, w_z, w_out, p0, *z_here, *z_there),
-        [SMEM] + [ANY] * 12,
+        [((both, width), BF16), ((both, width), BF16), ((width, depth), BF16)],
+        (core_s, tok, seen, y, w_z, w_out, *z_here, *z_there),
+        [SMEM] + [ANY] * 11,
         scratch=[pltpu.VMEM((depth, wide), BF16)],
         flops=2 * 10**9,
     )
-    ends = (core_s, back, seen, yg, eg, gains, wo)
+    ends = (core_s, back, seen, yg, eg, prm, wo)
     specs = [SMEM, VMEM, ANY, VMEM, VMEM, VMEM, VMEM]
     scratch = [pltpu.VMEM((length, width), BF16)]
     (away,) = call(final_send_kernel, [((length, depth), BF16)], ends, specs, scratch=scratch, flops=10**9)

time: 83.9 us -> 83.7 us (level)
  blocking collectives: 0 us -> 18.9 us
  starting transfers between devices: 44.3 us -> 29.4 us
  local copies, waits for them, and re-layouts: 9.98 us -> 5.23 us
  waiting for transfers between devices: 10.8 us -> 12.9 us
    all_to_all x0 -> x1, blocking collectives: none -> 18.9 us  [layer(): back = lax.all_to_all(carries, CHIPS, 0, 0)]
    all_to_all x1 -> x0, starting transfers between devices: 9.21 us -> none  [layer(): back = lax.all_to_all(carries, CHIPS, 0, 0)]
    ppermute x15, starting transfers between devices: 19 us -> 13.8 us  [around(): lax.ppermute(value, axis, [(k, (k + steps) % count) for k in range(count)])]
    unnamed x50 -> x22, local copies, waits for them, and re-layouts: 9.16 us -> 4.4 us
    ppermute x15, waiting for transfers between devices: 8.58 us -> 12.1 us  [around(): lax.ppermute(value, axis, [(k, (k + steps) % count) for k in range(count)])]
    all_to_all x1 -> x0, waiting for transfers between devices: 2.03 us -> none  [layer(): back = lax.all_to_all(carries, CHIPS, 0, 0)]
  transfers between devices with their start and end apart: 18 -> 17, of which waited for: 5 -> 5; matrix products, arithmetic and copies ran while one was open for 3% -> 2% of each run, Pallas kernels for 12% -> 11%
where the time goes in v1:
time: 83.7 us; the launch traced here: 83.4 us
  starting transfers between devices  29.4 us (35%)
  blocking collectives  18.9 us (23%)
  Pallas kernels  15.4 us (18%)
  waiting for transfers between devices  12.9 us (15%)
  local copies, waits for them, and re-layouts  5.23 us (6%)
  other arithmetic  1.06 us (1%)
    all_to_all x1, blocking collectives, layer(): back = lax.all_to_all(carries, CHIPS, 0, 0)  18.9 us
    pallas_call x9, Pallas kernels, call(): pl.pallas_call(kernel, out_shape=[jax.ShapeDtypeStruct(shape, dtype) for...  15.4 us
    ppermute x15, starting transfers between devices, around(): lax.ppermute(value, axis, [(k, (k + steps) % count) for k in range(count)])  13.8 us
    all_to_all x1, starting transfers between devices, layer(): arrived = lax.all_to_all(msg, CHIPS, 0, 0)  12.5 us
    ppermute x15, waiting for transfers between devices, around(): lax.ppermute(value, axis, [(k, (k + steps) % count) for k in range(count)])  12.1 us
    unnamed x22, local copies, waits for them, and re-layouts  4.4 us
    ppermute x1, starting transfers between devices, layer(): halo = lax.ppermute(edge, CHIPS, [(k, k + 1) for k in range(chips - 1)])  3.2 us
  transfers between devices with their start and end apart: 17, of which 5 were waited for; matrix products, arithmetic and copies ran while one was open for 2% of the time, Pallas kernels for 11%

profile of v1, /device:TPU:1, one launch (start us, length us, event | category | flops | bytes accessed | tf_op | source)
XLA Modules:
  0.0 83.4 jit_solution(12050951139199724721)
XLA Ops:
  0.0 3.2 %collective-permute-start = (bf16[2,256,512]{2,1,0:T(8,128)(2,1)}, bf16[2,256,512]{2,1,0:T(8,128)(2,1)S(1)}, u32[]{:S(2)}, u32[]{:S(2)}) collective-permute-start(bf16[2,256,512]{2,1,0:T(8,128)(2,1)} %tokens_ref.1), channel_id=1, source_target_pairs={{0,4},{4,0},{1,5},{5,1},{2,6},{6,2},{3,7},{7,3},{8,12},{12,8},{9,1... | collective-permute-start | bytes 1572872 | tf_op jit(solution)/shard_map/ppermute | solution.py:287
  3.2 0.7 broadcast_in_dim.15
  3.9 0.1 broadcast_in_dim_reshape.3
  4.0 0.6 copy-done.3
  4.6 1.0 %slice_select_fusion.2 = bf16[256,256]{1,0:T(8,128)(2,1)S(1)} fusion(bf16[512,256]{1,0:T(8,128)(2,1)} %w_ref.1, pred[]{:T(512)S(6)} %eq.3), kind=kLoop, calls=%fused_computation.4 | loop fusion | flops 65536 | bytes 393217 | tf_op jit(solution)/shard_map/jit(_where)/select_n | solution.py:313
  5.6 0.0 copy-start.6
  5.7 0.8 %collective-permute-start.5 = (bf16[264,256]{1,0:T(8,128)(2,1)S(1)}, bf16[264,256]{1,0:T(8,128)(2,1)S(1)}, u32[]{:S(2)}, u32[]{:S(2)}) collective-permute-start(bf16[264,256]{1,0:T(8,128)(2,1)S(1)} %pad_add_fusion.1), channel_id=1, source_target_pairs={{0,3},{1,0},{2,1},{3,2},{4,7},{5,4},{6,5},{7,6},{8,11},{9,8},{10,9... | collective-permute-start | bytes 405512 | tf_op jit(solution)/shard_map/ppermute | solution.py:287
  6.5 0.5 collective-permute-start.4
  7.0 0.6 collective-permute-start.3
  7.6 0.8 %collective-permute-start.1 = (bf16[2,16,256]{2,1,0:T(8,128)(2,1)S(1)}, bf16[2,16,256]{2,1,0:T(8,128)(2,1)S(1)}, u32[]{:S(2)}, u32[]{:S(2)}) collective-permute-start(bf16[2,16,256]{2,1,0:T(8,128)(2,1)S(1)} %bitcast.3), channel_id=1, source_target_pairs={{0,4},{4,0},{1,5},{5,1},{2,6},{6,2},{3,7},{7,3},{8,12},{12,8},{9,1... | collective-permute-start | bytes 49160 | tf_op jit(solution)/shard_map/ppermute | solution.py:287
  8.5 2.4 %collective-permute-done.5.rest_2_ = bf16[264,256]{1,0:T(8,128)(2,1)S(1)} collective-permute-done((bf16[264,256]{1,0:T(8,128)(2,1)S(1)}, bf16[264,256]{1,0:T(8,128)(2,1)S(1)}, u32[]{:S(2)}, u32[]{:S(2)}) %collective-permute-start.5) | collective-permute-done | bytes 135200 | tf_op jit(solution)/shard_map/ppermute | solution.py:287
  10.9 1.3 %collective-permute-start.8 = (bf16[264,256]{1,0:T(8,128)(2,1)S(1)}, bf16[264,256]{1,0:T(8,128)(2,1)S(1)}, u32[]{:S(2)}, u32[]{:S(2)}) collective-permute-start(bf16[264,256]{1,0:T(8,128)(2,1)S(1)} %collective-permute-done.5.rest_2_), channel_id=1, source_target_pairs={{0,4},{4,0},{1,5},{5,1},{2,6},{6,2},{3,7},{7,3},{8,12},{12,8},{9,1... | collective-permute-start | bytes 405512 | tf_op jit(solution)/shard_map/ppermute | solution.py:287
  12.2 0.7 collective-permute-done.4.rest_1_
  12.9 1.9 %collective-permute-start.7 = (bf16[264,256]{1,0:T(8,128)(2,1)S(1)}, bf16[264,256]{1,0:T(8,128)(2,1)S(1)}, u32[]{:S(2)}, u32[]{:S(2)}) collective-permute-start(bf16[264,256]{1,0:T(8,128)(2,1)S(1)} %collective-permute-done.4.rest_1_), channel_id=1, source_target_pairs={{0,4},{4,0},{1,5},{5,1},{2,6},{6,2},{3,7},{7,3},{8,12},{12,8},{9,1... | collective-permute-start | bytes 405512 | tf_op jit(solution)/shard_map/ppermute | solution.py:287
  14.8 1.6 %collective-permute-done.3.rest_0_ = bf16[264,256]{1,0:T(8,128)(2,1)S(1)} collective-permute-done((bf16[264,256]{1,0:T(8,128)(2,1)S(1)}, bf16[264,256]{1,0:T(8,128)(2,1)S(1)}, u32[]{:S(2)}, u32[]{:S(2)}) %collective-permute-start.3) | collective-permute-done | bytes 135200 | tf_op jit(solution)/shard_map/ppermute | solution.py:287
  16.4 0.5 collective-permute-start.6
  16.9 0.0 copy-start
  16.9 0.0 copy-start.5
  17.0 0.9 %shard_map.100 = (bf16[512,512]{1,0:T(8,128)(2,1)S(1)}, bf16[16,512]{1,0:T(8,128)(2,1)S(1)}, bf16[512,128]{1,0:T(8,128)(2,1)S(1)}, bf16[512,256]{1,0:T(8,128)(2,1)S(1)}, bf16[8,1024]{1,0:T(8,128)(2,1)S(1)}) custom-call(s32[1]{0:T(128)} %bitcast.c_ref, s32[1]{0:T(128)} %bitcast.1.x_ref, bf16[2,256,512]{2,1,0:T(8,128)(2,1)S(1)} %copy-done.4, ...), custom_call_target="tpu_custom_call" | custom-call | flops 1000000000 | bytes 1048576 | tf_op jit(solution)/shard_map/pallas_call | solution.py:274
  17.9 3.2 %collective-permute-start.2 = (bf16[16,512]{1,0:T(8,128)(2,1)S(1)}, bf16[16,512]{1,0:T(8,128)(2,1)S(1)}, u32[]{:S(2)}, u32[]{:S(2)}) collective-permute-start(bf16[16,512]{1,0:T(8,128)(2,1)S(1)} %get-tuple-element.30), channel_id=1, source_target_pairs={{0,8},{8,16},{16,24},{24,32},{32,40},{40,48},{48,56},{56,64},{64,7... | collective-permute-start | bytes 49160 | tf_op jit(solution)/shard_map/ppermute | solution.py:331
  21.1 0.9 %collective-permute-done.2.halo_ref = bf16[16,512]{1,0:T(8,128)(2,1)S(1)} collective-permute-done((bf16[16,512]{1,0:T(8,128)(2,1)S(1)}, bf16[16,512]{1,0:T(8,128)(2,1)S(1)}, u32[]{:S(2)}, u32[]{:S(2)}) %collective-permute-start.2) | collective-permute-done | bytes 16416 | tf_op jit(solution)/shard_map/ppermute | solution.py:331
  22.0 0.7 copy-done.7
  22.6 1.0 %shard_map.101 = (bf16[512,128]{1,0:T(8,128)(2,1)S(1)}, bf16[128,512]{1,0:T(8,128)(2,1)S(1)}, bf16[512,256]{1,0:T(8,128)(2,1)S(1)}, bf16[32,24,128]{2,1,0:T(8,128)(2,1)S(1)}) custom-call(bf16[512,512]{1,0:T(8,128)(2,1)S(1)} %get-tuple-element.29.tok_ref, bf16[16,512]{1,0:T(8,128)(2,1)S(1)} %collective-permute-done.2.halo_ref, ...), custom_call_target="tpu_custom_call" | custom-call | flops 1000000000 | bytes 1048576 | tf_op jit(solution)/shard_map/pallas_call | solution.py:274
  23.7 0.0 collective-permute-done.8.rest_5_
  23.7 0.0 collective-permute-done.6.rest_3_
  23.7 2.6 %shard_map.102 = (bf16[512,768]{1,0:T(8,128)(2,1)S(1)}, bf16[32,24,128]{2,1,0:T(8,128)(2,1)}, bf16[512,256]{1,0:T(8,128)(2,1)S(1)}, bf16[8,1024]{1,0:T(8,128)(2,1)S(1)}) custom-call(s32[1]{0:T(128)} %bitcast.c_ref, bf16[512,512]{1,0:T(8,128)(2,1)S(1)} %get-tuple-element.29.tok_ref, bf16[16,512]{1,0:T(8,128)(2,1)S(1)} %collective-permute-done.2.halo_ref, ...), custom_call_target="tpu_custom_call" | custom-call | flops 1000000000 | bytes 1048576 | tf_op jit(solution)/shard_map/pallas_call | solution.py:274
  26.3 12.5 %all-to-all-start = ((bf16[32,24,128]{2,1,0:T(8,128)(2,1)}), bf16[32,24,128]{2,1,0:T(8,128)(2,1)S(1)}, u32[]{:S(2)}, u32[]{:S(2)}) async-start(bf16[32,24,128]{2,1,0:T(8,128)(2,1)} %get-tuple-element.37), calls=%async_computation | async-start | bytes 393216 | tf_op jit(solution)/shard_map/all_to_all | solution.py:348
  38.8 0.0 copy-start.2
  38.8 0.9 %copy-done.2 = bf16[256,512]{1,0:T(8,128)(2,1)S(1)} copy-done((bf16[256,512]{1,0:T(8,128)(2,1)S(1)}, bf16[256,512]{1,0:T(8,128)(2,1)}, u32[]{:S(2)}) %copy-start.2) | copy-done | bytes 262168
  39.8 0.4 collective-permute-start.11
  40.2 0.5 collective-permute-start.10
  40.7 0.7 collective-permute-start.9
  41.4 5.9 %shard_map.103.y_ref = bf16[512,1024]{1,0:T(8,128)(2,1)S(1)} custom-call(bf16[512,256]{1,0:T(8,128)(2,1)S(1)} %get-tuple-element.40.xa0_ref, bf16[512,768]{1,0:T(8,128)(2,1)S(1)} %get-tuple-element.41.xa1_ref, bf16[512,256]{1,0:T(8,128)(2,1)S(1)} %get-tuple-element.42.seen_ref, bf16[8,1024]{1,0:T(8,128)(2,1)S(1)} %get-tuple-element.43.prm_ref.gain_ref), custom_call_target="tpu_custom_call" | custom-call | flops 2000000000 | bytes 1048576 | tf_op jit(solution)/shard_map/pallas_call | solution.py:274
  47.3 1.0 %copy-done.8 = bf16[512,1024]{1,0:T(8,128)(2,1)} copy-done((bf16[512,1024]{1,0:T(8,128)(2,1)}, bf16[512,1024]{1,0:T(8,128)(2,1)S(1)}, u32[]{:S(2)}) %copy-start.8) | copy-done | bytes 1048600
  48.3 0.0 collective-permute-done.11.rest_2_
  48.3 0.0 collective-permute-done.10.rest_1_
  48.3 7.3 %collective-permute-done.9.rest_0_ = bf16[512,256]{1,0:T(8,128)(2,1)S(1)} collective-permute-done((bf16[512,256]{1,0:T(8,128)(2,1)S(1)}, bf16[512,256]{1,0:T(8,128)(2,1)S(1)}, u32[]{:S(2)}, u32[]{:S(2)}) %collective-permute-start.9) | collective-permute-done | bytes 262176 | tf_op jit(solution)/shard_map/ppermute | solution.py:287
  55.6 0.5 collective-permute-start.12
  56.1 0.0 collective-permute-start.13
  56.1 0.5 collective-permute-start.14
  56.6 0.1 shard_map.104
  56.7 18.9 %all_to_all.10.back_ref = bf16[32,16,128]{2,1,0:T(8,128)(2,1)S(1)} all-to-all(bf16[32,16,128]{2,1,0:T(8,128)(2,1)S(1)} %shard_map.104), channel_id=1, replica_groups=mesh['seq_0'=8,'seq_1'=4,'seq_2'=2,'mix'=4] {'seq_0','seq_1'}, dimensions={0} | all-to-all | bytes 262144 | tf_op jit(solution)/shard_map/all_to_all | solution.py:359
  75.6 1.2 %copy-done.9 = bf16[512,1024]{1,0:T(8,128)(2,1)S(1)} copy-done((bf16[512,1024]{1,0:T(8,128)(2,1)S(1)}, bf16[512,1024]{1,0:T(8,128)(2,1)}, u32[]{:S(2)}) %copy-start.9) | copy-done | bytes 1048600
  76.9 1.3 %shard_map.105 = (bf16[512,1024]{1,0:T(8,128)(2,1)S(1)}, bf16[512,1024]{1,0:T(8,128)(2,1)S(1)}, bf16[1024,512]{1,0:T(8,128)(2,1)S(1)}) custom-call(s32[1]{0:T(128)} %bitcast.c_ref, bf16[512,512]{1,0:T(8,128)(2,1)S(1)} %get-tuple-element.29.tok_ref, bf16[512,256]{1,0:T(8,128)(2,1)S(1)} %get-tuple-element.42.seen_ref, bf16[512,1024]{1,0:T(8,128)(2,1)S(1)} %copy-done.9, ...), custom_call_target="tpu_custom_call" | custom-call | flops 2000000000 | bytes 1048576 | tf_op jit(solution)/shard_map/pallas_call | solution.py:274
  78.2 1.4 %shard_map.107 = bf16[256,512]{1,0:T(8,128)(2,1)S(1)} custom-call(s32[1]{0:T(128)} %bitcast.c_ref, bf16[32,16,128]{2,1,0:T(8,128)(2,1)S(1)} %all_to_all.10.back_ref, bf16[512,256]{1,0:T(8,128)(2,1)S(1)} %get-tuple-element.42.seen_ref, bf16[512,1024]{1,0:T(8,128)(2,1)S(1)} %get-tuple-element.50.yg_ref, bf16[512,1024]{1,0:T(8,128)(2,1)S(1)} %get-tuple-element.51.eg_ref, ...), custom_call_target="tpu_custom_call" | custom-call | flops 1000000000 | bytes 1048576 | tf_op jit(solution)/shard_map/pallas_call | solution.py:274
  79.5 1.5 %collective-permute-start.15 = (bf16[256,512]{1,0:T(8,128)(2,1)S(1)}, bf16[256,512]{1,0:T(8,128)(2,1)S(1)}, u32[]{:S(2)}, u32[]{:S(2)}) collective-permute-start(bf16[256,512]{1,0:T(8,128)(2,1)S(1)} %shard_map.107), channel_id=1, source_target_pairs={{0,4},{4,0},{1,5},{5,1},{2,6},{6,2},{3,7},{7,3},{8,12},{12,8},{9,1... | collective-permute-start | bytes 786440 | tf_op jit(solution)/shard_map/ppermute | solution.py:287
  81.1 1.4 %shard_map.106.own_ref = bf16[256,512]{1,0:T(8,128)(2,1)S(1)} custom-call(s32[1]{0:T(128)} %bitcast.c_ref, bf16[32,16,128]{2,1,0:T(8,128)(2,1)S(1)} %all_to_all.10.back_ref, bf16[512,256]{1,0:T(8,128)(2,1)S(1)} %get-tuple-element.42.seen_ref, bf16[512,1024]{1,0:T(8,128)(2,1)S(1)} %get-tuple-element.50.yg_ref, ...), custom_call_target="tpu_custom_call" | custom-call | flops 1000000000 | bytes 1048576 | tf_op jit(solution)/shard_map/pallas_call | solution.py:274
  82.4 0.8 shard_map.108
  (28 shorter events, 0.1 us)
Async XLA Ops:
  0.0 16.9 %collective-permute-start = (bf16[2,256,512]{2,1,0:T(8,128)(2,1)}, bf16[2,256,512]{2,1,0:T(8,128)(2,1)S(1)}, u32[]{:S(2)}, u32[]{:S(2)}) collective-permute-start(bf16[2,256,512]{2,1,0:T(8,128)(2,1)} %tokens_ref.1), channel_id=1, source_target_pairs={{0,4},{4,0},{1,5},{5,1},{2,6},{6,2},{3,7},{7,3},{8,12},{12,8},{9,1... | collective-permute-start | bytes 1572872 | tf_op jit(solution)/shard_map/ppermute | solution.py:287
  3.2 0.8 copy-start.10
  3.9 0.7 copy-start.3
  3.9 13.0 %copy-start.4 = (bf16[2,256,512]{2,1,0:T(8,128)(2,1)S(1)}, bf16[2,256,512]{2,1,0:T(8,128)(2,1)}, u32[]{:S(2)}) copy-start(bf16[2,256,512]{2,1,0:T(8,128)(2,1)} %tokens_ref.1) | copy-start | bytes 1572868
  5.6 2.0 %copy-start.6 = (bf16[2,256,16]{1,2,0:T(8,128)(2,1)S(1)}, bf16[2,256,16]{1,2,0:T(8,128)(2,1)}, u32[]{:S(2)}) copy-start(bf16[2,256,16]{1,2,0:T(8,128)(2,1)} %param.11) | copy-start | bytes 49156
  5.7 5.2 %collective-permute-start.5 = (bf16[264,256]{1,0:T(8,128)(2,1)S(1)}, bf16[264,256]{1,0:T(8,128)(2,1)S(1)}, u32[]{:S(2)}, u32[]{:S(2)}) collective-permute-start(bf16[264,256]{1,0:T(8,128)(2,1)S(1)} %pad_add_fusion.1), channel_id=1, source_target_pairs={{0,3},{1,0},{2,1},{3,2},{4,7},{5,4},{6,5},{7,6},{8,11},{9,8},{10,9... | collective-permute-start | bytes 405512 | tf_op jit(solution)/shard_map/ppermute | solution.py:287
  6.5 6.4 %collective-permute-start.4 = (bf16[264,256]{1,0:T(8,128)(2,1)S(1)}, bf16[264,256]{1,0:T(8,128)(2,1)S(1)}, u32[]{:S(2)}, u32[]{:S(2)}) collective-permute-start(bf16[264,256]{1,0:T(8,128)(2,1)S(1)} %pad_add_fusion.1), channel_id=1, source_target_pairs={{0,2},{1,3},{2,0},{3,1},{4,6},{5,7},{6,4},{7,5},{8,10},{9,11},{10,... | collective-permute-start | bytes 405512 | tf_op jit(solution)/shard_map/ppermute | solution.py:287
  7.0 9.4 %collective-permute-start.3 = (bf16[264,256]{1,0:T(8,128)(2,1)S(1)}, bf16[264,256]{1,0:T(8,128)(2,1)S(1)}, u32[]{:S(2)}, u32[]{:S(2)}) collective-permute-start(bf16[264,256]{1,0:T(8,128)(2,1)S(1)} %pad_add_fusion.1), channel_id=1, source_target_pairs={{0,1},{1,2},{2,3},{3,0},{4,5},{5,6},{6,7},{7,4},{8,9},{9,10},{10,1... | collective-permute-start | bytes 405512 | tf_op jit(solution)/shard_map/ppermute | solution.py:287
  7.6 9.3 %collective-permute-start.1 = (bf16[2,16,256]{2,1,0:T(8,128)(2,1)S(1)}, bf16[2,16,256]{2,1,0:T(8,128)(2,1)S(1)}, u32[]{:S(2)}, u32[]{:S(2)}) collective-permute-start(bf16[2,16,256]{2,1,0:T(8,128)(2,1)S(1)} %bitcast.3), channel_id=1, source_target_pairs={{0,4},{4,0},{1,5},{5,1},{2,6},{6,2},{3,7},{7,3},{8,12},{12,8},{9,1... | collective-permute-start | bytes 49160 | tf_op jit(solution)/shard_map/ppermute | solution.py:287
  10.9 12.8 %collective-permute-start.8 = (bf16[264,256]{1,0:T(8,128)(2,1)S(1)}, bf16[264,256]{1,0:T(8,128)(2,1)S(1)}, u32[]{:S(2)}, u32[]{:S(2)}) collective-permute-start(bf16[264,256]{1,0:T(8,128)(2,1)S(1)} %collective-permute-done.5.rest_2_), channel_id=1, source_target_pairs={{0,4},{4,0},{1,5},{5,1},{2,6},{6,2},{3,7},{7,3},{8,12},{12,8},{9,1... | collective-permute-start | bytes 405512 | tf_op jit(solution)/shard_map/ppermute | solution.py:287
  12.9 10.8 %collective-permute-start.7 = (bf16[264,256]{1,0:T(8,128)(2,1)S(1)}, bf16[264,256]{1,0:T(8,128)(2,1)S(1)}, u32[]{:S(2)}, u32[]{:S(2)}) collective-permute-start(bf16[264,256]{1,0:T(8,128)(2,1)S(1)} %collective-permute-done.4.rest_1_), channel_id=1, source_target_pairs={{0,4},{4,0},{1,5},{5,1},{2,6},{6,2},{3,7},{7,3},{8,12},{12,8},{9,1... | collective-permute-start | bytes 405512 | tf_op jit(solution)/shard_map/ppermute | solution.py:287
  16.4 7.3 %collective-permute-start.6 = (bf16[264,256]{1,0:T(8,128)(2,1)S(1)}, bf16[264,256]{1,0:T(8,128)(2,1)S(1)}, u32[]{:S(2)}, u32[]{:S(2)}) collective-permute-start(bf16[264,256]{1,0:T(8,128)(2,1)S(1)} %collective-permute-done.3.rest_0_), channel_id=1, source_target_pairs={{0,4},{4,0},{1,5},{5,1},{2,6},{6,2},{3,7},{7,3},{8,12},{12,8},{9,1... | collective-permute-start | bytes 405512 | tf_op jit(solution)/shard_map/ppermute | solution.py:287
  16.9 5.0 %copy-start = (bf16[512,256]{1,0:T(8,128)(2,1)S(1)}, bf16[512,256]{1,0:T(8,128)(2,1)}, u32[]{:S(2)}) copy-start(bf16[512,256]{1,0:T(8,128)(2,1)} %w_ref.1) | copy-start | bytes 786436
  16.9 5.0 %copy-start.5 = (bf16[512,128]{1,0:T(8,128)(2,1)S(1)}, bf16[512,128]{1,0:T(8,128)(2,1)}, u32[]{:S(2)}) copy-start(bf16[512,128]{1,0:T(8,128)(2,1)} %wbc_ref.1) | copy-start | bytes 393220
  17.9 4.1 %collective-permute-start.2 = (bf16[16,512]{1,0:T(8,128)(2,1)S(1)}, bf16[16,512]{1,0:T(8,128)(2,1)S(1)}, u32[]{:S(2)}, u32[]{:S(2)}) collective-permute-start(bf16[16,512]{1,0:T(8,128)(2,1)S(1)} %get-tuple-element.30), channel_id=1, source_target_pairs={{0,8},{8,16},{16,24},{24,32},{32,40},{40,48},{48,56},{56,64},{64,7... | collective-permute-start | bytes 49160 | tf_op jit(solution)/shard_map/ppermute | solution.py:331
  22.0 0.7 copy-start.7
  26.3 12.5 %copy-start.1 = (bf16[512,256]{1,0:T(8,128)(2,1)S(1)}, bf16[512,256]{1,0:T(8,128)(2,1)}, u32[]{:S(2)}) copy-start(bf16[512,256]{1,0:T(8,128)(2,1)} %wz0_ref) | copy-start | bytes 786436
  26.3 30.2 %all-to-all-start = ((bf16[32,24,128]{2,1,0:T(8,128)(2,1)}), bf16[32,24,128]{2,1,0:T(8,128)(2,1)S(1)}, u32[]{:S(2)}, u32[]{:S(2)}) async-start(bf16[32,24,128]{2,1,0:T(8,128)(2,1)} %get-tuple-element.37), calls=%async_computation | async-start | bytes 393216 | tf_op jit(solution)/shard_map/all_to_all | solution.py:348
  38.8 1.0 %copy-start.2 = (bf16[256,512]{1,0:T(8,128)(2,1)S(1)}, bf16[256,512]{1,0:T(8,128)(2,1)}, u32[]{:S(2)}) copy-start(bf16[256,512]{1,0:T(8,128)(2,1)} %wo0_ref) | copy-start | bytes 786436
  39.8 8.4 %collective-permute-start.11 = (bf16[512,256]{1,0:T(8,128)(2,1)S(1)}, bf16[512,256]{1,0:T(8,128)(2,1)S(1)}, u32[]{:S(2)}, u32[]{:S(2)}) collective-permute-start(bf16[512,256]{1,0:T(8,128)(2,1)S(1)} %pad_add_fusion), channel_id=1, source_target_pairs={{0,3},{1,0},{2,1},{3,2},{4,7},{5,4},{6,5},{7,6},{8,11},{9,8},{10,9... | collective-permute-start | bytes 786440 | tf_op jit(solution)/shard_map/ppermute | solution.py:287
  40.2 8.1 %collective-permute-start.10 = (bf16[512,256]{1,0:T(8,128)(2,1)S(1)}, bf16[512,256]{1,0:T(8,128)(2,1)S(1)}, u32[]{:S(2)}, u32[]{:S(2)}) collective-permute-start(bf16[512,256]{1,0:T(8,128)(2,1)S(1)} %pad_add_fusion), channel_id=1, source_target_pairs={{0,2},{1,3},{2,0},{3,1},{4,6},{5,7},{6,4},{7,5},{8,10},{9,11},{10,... | collective-permute-start | bytes 786440 | tf_op jit(solution)/shard_map/ppermute | solution.py:287
  40.7 14.9 %collective-permute-start.9 = (bf16[512,256]{1,0:T(8,128)(2,1)S(1)}, bf16[512,256]{1,0:T(8,128)(2,1)S(1)}, u32[]{:S(2)}, u32[]{:S(2)}) collective-permute-start(bf16[512,256]{1,0:T(8,128)(2,1)S(1)} %pad_add_fusion), channel_id=1, source_target_pairs={{0,1},{1,2},{2,3},{3,0},{4,5},{5,6},{6,7},{7,4},{8,9},{9,10},{10,1... | collective-permute-start | bytes 786440 | tf_op jit(solution)/shard_map/ppermute | solution.py:287
  47.3 1.0 %copy-start.8 = (bf16[512,1024]{1,0:T(8,128)(2,1)}, bf16[512,1024]{1,0:T(8,128)(2,1)S(1)}, u32[]{:S(2)}) copy-start(bf16[512,1024]{1,0:T(8,128)(2,1)S(1)} %shard_map.103.y_ref) | copy-start | bytes 3145732
  55.6 20.1 %collective-permute-start.12 = (bf16[512,256]{1,0:T(8,128)(2,1)S(1)}, bf16[512,256]{1,0:T(8,128)(2,1)S(1)}, u32[]{:S(2)}, u32[]{:S(2)}) collective-permute-start(bf16[512,256]{1,0:T(8,128)(2,1)S(1)} %collective-permute-done.9.rest_0_), channel_id=1, source_target_pairs={{0,4},{4,0},{1,5},{5,1},{2,6},{6,2},{3,7},{7,3},{8,12},{12,8},{9,1... | collective-permute-start | bytes 786440 | tf_op jit(solution)/shard_map/ppermute | solution.py:287
  56.1 19.6 %collective-permute-start.13 = (bf16[512,256]{1,0:T(8,128)(2,1)S(1)}, bf16[512,256]{1,0:T(8,128)(2,1)S(1)}, u32[]{:S(2)}, u32[]{:S(2)}) collective-permute-start(bf16[512,256]{1,0:T(8,128)(2,1)S(1)} %collective-permute-done.10.rest_1_), channel_id=1, source_target_pairs={{0,4},{4,0},{1,5},{5,1},{2,6},{6,2},{3,7},{7,3},{8,12},{12,8},{9,1... | collective-permute-start | bytes 786440 | tf_op jit(solution)/shard_map/ppermute | solution.py:287
  56.1 19.6 %collective-permute-start.14 = (bf16[512,256]{1,0:T(8,128)(2,1)S(1)}, bf16[512,256]{1,0:T(8,128)(2,1)S(1)}, u32[]{:S(2)}, u32[]{:S(2)}) collective-permute-start(bf16[512,256]{1,0:T(8,128)(2,1)S(1)} %collective-permute-done.11.rest_2_), channel_id=1, source_target_pairs={{0,4},{4,0},{1,5},{5,1},{2,6},{6,2},{3,7},{7,3},{8,12},{12,8},{9,1... | collective-permute-start | bytes 786440 | tf_op jit(solution)/shard_map/ppermute | solution.py:287
  75.6 1.2 %copy-start.9 = (bf16[512,1024]{1,0:T(8,128)(2,1)S(1)}, bf16[512,1024]{1,0:T(8,128)(2,1)}, u32[]{:S(2)}) copy-start(bf16[512,1024]{1,0:T(8,128)(2,1)} %copy-done.8) | copy-start | bytes 3145732
  79.5 2.9 %collective-permute-start.15 = (bf16[256,512]{1,0:T(8,128)(2,1)S(1)}, bf16[256,512]{1,0:T(8,128)(2,1)S(1)}, u32[]{:S(2)}, u32[]{:S(2)}) collective-permute-start(bf16[256,512]{1,0:T(8,128)(2,1)S(1)} %shard_map.107), channel_id=1, source_target_pairs={{0,4},{4,0},{1,5},{5,1},{2,6},{6,2},{3,7},{7,3},{8,12},{12,8},{9,1... | collective-permute-start | bytes 786440 | tf_op jit(solution)/shard_map/ppermute | solution.py:287

commit v2 on v1

--- a/solution.py
+++ b/solution.py
@@ -16,6 +16,7 @@
 LANES = 128
 HALO = 16
 SHARDS = 4
+HEADS = 16
 PART = 16
 
 
@@ -31,19 +32,26 @@
     return jnp.where(mask, 1.0, 0.0).astype(BF16)
 
 
-def hi_lo(value):
+def two_terms(value):
     high = value.astype(BF16)
     low = (value - high.astype(F32)).astype(BF16)
     return jnp.concatenate([high, low], axis=-1)
 
 
+def hi_lo(value):
+    value = jnp.where(iota(value.shape, 1) < HEADS, value, 0.0)
+    high = value.astype(BF16).astype(F32)
+    return (high + pltpu.roll(value - high, HEADS, 1)).astype(BF16)
+
+
 def lower_ones(size):
     return ones_where(iota((size, size), 0) >= iota((size, size), 1))
 
 
 def spread(start, width):
-    shape = (2 * LANES, width)
-    return ones_where((iota(shape, 0) & (LANES - 1)) == ((iota(shape, 1) + start) >> 6))
+    shape = (LANES, width)
+    row = iota(shape, 0)
+    return ones_where(((row & (HEADS - 1)) == ((iota(shape, 1) + start) >> 6)) & (row < 2 * HEADS))
 
 
 def scale_of(rate):
@@ -79,14 +87,13 @@
             msg_ref[at_piece, 0:PART] = state[q * PART : (q + 1) * PART, p * LANES : (p + 1) * LANES]
 
 
-def decay_kernel(c_ref, x_ref, tokens_ref, log_ref, got_ref, got_log_ref, tok_ref, edge_ref, logp_ref, tail_ref, extra_ref):
+def decay_kernel(c_ref, x_ref, tokens_ref, log_ref, got_ref, got_log_ref, tok_ref, logp_ref, tail_ref, extra_ref):
     core, mine = c_ref[0], x_ref[0]
     heads, length = log_ref.shape[1:]
     here = pl.multiple_of(core * length, length)
     there = pl.multiple_of((1 - core) * length, length)
     tok_ref[pl.ds(here, length)] = tokens_ref[core]
     tok_ref[pl.ds(there, length)] = got_ref[core]
-    edge_ref[...] = tok_ref[2 * length - HALO :]
     per = heads // SHARDS
     shape = (LANES, heads)
     rel = iota(shape, 0)
@@ -108,19 +115,22 @@
 
 
 def own_kernel(
-    tok_ref, halo_ref, tail_ref, extra_ref, wbc_ref, cbc_ref, w_ref, cx_ref,
-    bc_ref, bt_ref, xa_ref, msg_ref,
+    c_ref, tok_ref, h0_ref, h1_ref, tail_ref, extra_ref, wbc_ref, w_ref, prm_ref,
+    halo_ref, bc_ref, bt_ref, xa_ref, msg_ref,
 ):
+    core = c_ref[0]
+    halo_ref[...] = h0_ref[core] + h1_ref[core]
     extra = extra_ref[...]
     parts = STATE // PART
     for j in range(extra.shape[1] // LANES):
         for q in range(parts):
             msg_ref[j * parts + q, PART : PART + 8] = extra[:, j * LANES : (j + 1) * LANES]
-    taps = cbc_ref[...].astype(F32)
+    prm = prm_ref[...].astype(F32)
+    taps = prm[8 : 8 + CONV, 0 : 2 * STATE]
     bc = conv_silu(dot(halo_ref[...], wbc_ref[...]), dot(tok_ref[...], wbc_ref[...]), taps)
     bc_ref[...] = bc
     bt_ref[...] = bc.astype(F32).T.astype(BF16)
-    shard_states(w_ref[...], cx_ref[...].astype(F32), 0, 0, tok_ref, halo_ref, tail_ref, bt_ref, xa_ref, msg_ref)
+    shard_states(w_ref[...], prm[0:CONV], 0, 0, tok_ref, halo_ref, tail_ref, bt_ref, xa_ref, msg_ref)
 
 
 def others_kernel(c_ref, tok_ref, halo_ref, tail_ref, bt_ref, bc_ref, logp_ref, own_msg_ref, own_prm_ref, *rest):
@@ -131,7 +141,7 @@
     seen_ref[:, LANES:] = logp_ref[...]
     half, wide = w_ref.shape[0] // 2, w_ref.shape[1]
     msg_ref[...] = own_msg_ref[...]
-    prm_ref[:, 0:wide] = own_prm_ref[...]
+    prm_ref[:, 0:wide] = own_prm_ref[0:8]
     for r in range(1, SHARDS):
         a, b = here[r - 1][0:half], there[r - 1][0:half]
         w_ref[0:half] = jnp.where(core == 0, a, b)
@@ -167,12 +177,16 @@
     reads = [bc[span[b]][:, STATE:] for b in range(blocks)]
     writes_t = [bt[0:STATE, b * BLOCK : (b + 1) * BLOCK] for b in range(blocks)]
     scores = [jnp.where(keep, dot(reads[b], writes_t[b]), 0.0) for b in range(blocks)]
-    enter = [hi_lo(jnp.exp(cum)) for cum in cums]
-    leave = [hi_lo(jnp.exp(cums[b][BLOCK - 1 :] - cums[b]) * scale[span[b]]) for b in range(blocks)]
-    last = [hi_lo(jnp.broadcast_to(jnp.exp(cums[b][BLOCK - 1 :]), (8, LANES))) for b in range(blocks)]
+    factors = hi_lo(
+        jnp.concatenate(
+            [jnp.exp(cum) for cum in cums[1:]]
+            + [jnp.exp(cums[b][BLOCK - 1 :] - cums[b]) * scale[span[b]] for b in range(blocks - 1)],
+            axis=0,
+        )
+    )
     for j in range(SHARDS * wide // LANES):
         lanes = slice(j * LANES, (j + 1) * LANES)
-        to_lanes = spread(j * LANES, LANES)
+        spreads = dot(factors, spread(j * LANES, LANES))
         skip = prm_ref[CONV + 1 : CONV + 2, lanes].astype(F32)
         state = None
         for b in range(blocks):
@@ -190,11 +204,12 @@
             split = jnp.concatenate([jnp.where(left, xb, zero), jnp.where(left, zero, xb)], axis=0)
             y = dot(jnp.concatenate(parts, axis=1), split) + skip * xb.astype(F32)
             if state is not None:
-                y = y + dot(enter[b], to_lanes) * dot(reads[b], state.astype(BF16))
+                enter = spreads[(b - 1) * BLOCK : b * BLOCK]
+                y = y + enter * dot(reads[b], state.astype(BF16))
             if b + 1 < blocks:
-                scaled = (xb.astype(F32) * dot(leave[b], to_lanes)).astype(BF16)
-                fresh = dot(writes_t[b], scaled)
-                state = fresh if state is None else fresh + dot(last[b], to_lanes)[0:1] * state
+                leave = spreads[(blocks - 1 + b) * BLOCK : (blocks + b) * BLOCK]
+                fresh = dot(writes_t[b], (xb.astype(F32) * leave).astype(BF16))
+                state = fresh if state is None else fresh + enter[BLOCK - 1 :] * state
             y_ref[span[b], lanes] = y.astype(BF16)
 
 
@@ -236,7 +251,7 @@
         lanes = slice(j * LANES, (j + 1) * LANES)
         carry = jnp.concatenate([back_ref[j * parts + q] for q in range(parts)], axis=0)
         v = yg_ref[rows, lanes].astype(F32) + eg_ref[rows, lanes].astype(F32) * dot(read, carry)
-        mean = dot(hi_lo(v * v), same_head) * (1.0 / 64.0)
+        mean = dot(two_terms(v * v), same_head) * (1.0 / 64.0)
         gain = gain_ref[CONV : CONV + 1, lanes].astype(F32)
         normed_ref[:, lanes] = (v * lax.rsqrt(mean + 1e-05) * gain).astype(BF16)
     return dot(normed_ref[...], wo_ref[...]).astype(BF16)
@@ -308,32 +323,41 @@
 
     low = core == 0
     extra = (
-        padded(conv_x, 0, 8) + padded(gain[None], CONV, 8) + padded(jnp.repeat(skip, wide // skip.shape[0])[None], CONV + 1, 8)
-    )
-    first = padded(jnp.where(low, w_x[:half], w_x[half:]), 0, half + 8) + padded(extra, half, half + 8)
+        padded(conv_x, 0, 16)
+        + padded(gain[None], CONV, 16)
+        + padded(jnp.repeat(skip, wide // skip.shape[0])[None], CONV + 1, 16)
+        + padded(conv_bc, 8, 16, wide)
+    )
+    first = padded(jnp.where(low, w_x[:half], w_x[half:]), 0, half + 16) + padded(extra, half, half + 16)
     x_here = [around(first, "mix", r) for r in (2, 1, 3)]
     x_here = [x_here[1], x_here[0], x_here[2]]
     got = around(tokens, "seq_2", 1)
     got_log = around(logs, "seq_2", 1)
-    tok, edge, logp, tail, totals = call(
+    edge = tokens[:, length - HALO :]
+    halo = [lax.ppermute(edge, SEQ, [(2 * k + 1, 2 * k + 2 + to) for k in range(chips - 1)]) for to in range(2)]
+    tok, logp, tail, totals = call(
         decay_kernel,
         [
             ((both, depth), BF16),
-            ((HALO, depth), BF16),
             ((both, LANES), BF16),
-            ((both, 2 * LANES), BF16),
+            ((both, LANES), BF16),
             ((8, width), BF16),
         ],
         (core_s, across_s, tokens, logs, got, got_log),
         [SMEM, SMEM, ANY, ANY, VMEM, VMEM],
         flops=10**9,
     )
-    halo = lax.ppermute(edge, CHIPS, [(k, k + 1) for k in range(chips - 1)])
-    bc, bt, xa0, own_msg = call(
+    halo, bc, bt, xa0, own_msg = call(
         own_kernel,
-        [((both, 2 * STATE), BF16), ((2 * STATE, both), BF16), ((both, wide), BF16), ((parts, PART + 8, LANES), BF16)],
-        (tok, halo, tail, totals, w_bc, conv_bc, w_x, conv_x),
-        [VMEM] * 4 + [ANY] * 4,
+        [
+            ((HALO, depth), BF16),
+            ((both, 2 * STATE), BF16),
+            ((2 * STATE, both), BF16),
+            ((both, wide), BF16),
+            ((parts, PART + 8, LANES), BF16),
+        ],
+        (core_s, tok, *halo, tail, totals, w_bc, w_x, extra),
+        [SMEM] + [VMEM] * 5 + [ANY] * 2 + [VMEM],
         flops=10**9,
     )
     x_there = [around(part, "seq_2", 1) for part in x_here]

time: 83.7 us -> 81.6 us (0.975)
  waiting for transfers between devices: 12.9 us -> 9.47 us
  starting transfers between devices: 29.4 us -> 31.8 us
  Pallas kernels: 15.4 us -> 14.1 us
    ppermute x1 -> x2, starting transfers between devices: 3.2 us -> 7.09 us  [layer(): lax.ppermute(edge, SEQ, [(2 * k + 1, 2 * k + 2 + to) for k in range(chips...]
    ppermute x15, waiting for transfers between devices: 12.1 us -> 9.46 us  [around(): lax.ppermute(value, axis, [(k, (k + steps) % count) for k in range(count)])]
    pallas_call x9, Pallas kernels: 15.4 us -> 14.1 us  [call(): pl.pallas_call(kernel, out_shape=[jax.ShapeDtypeStruct(shape, dtype) for...]
    all_to_all x1, starting transfers between devices: 12.5 us -> 11.2 us  [layer(): arrived = lax.all_to_all(msg, CHIPS, 0, 0)]
    unnamed x22 -> x16, local copies, waits for them, and re-layouts: 4.4 us -> 3.22 us
    ppermute x1 -> x2, waiting for transfers between devices: 0.85 us -> 0.01 us  [layer(): lax.ppermute(edge, SEQ, [(2 * k + 1, 2 * k + 2 + to) for k in range(chips...]
  transfers between devices with their start and end apart: 17 -> 18, of which waited for: 5 -> 3; matrix products, arithmetic and copies ran while one was open for 2% -> 4% of each run, Pallas kernels for 11% -> 10%
where the time goes in v2:
time: 81.6 us; the launch traced here: 81.2 us
  starting transfers between devices  31.8 us (39%)
  blocking collectives  18.9 us (23%)
  Pallas kernels  14.1 us (17%)
  waiting for transfers between devices  9.47 us (12%)
  local copies, waits for them, and re-layouts  4.7 us (6%)
  other arithmetic  1.76 us (2%)
    all_to_all x1, blocking collectives, layer(): back = lax.all_to_all(carries, CHIPS, 0, 0)  18.9 us
    pallas_call x9, Pallas kernels, call(): pl.pallas_call(kernel, out_shape=[jax.ShapeDtypeStruct(shape, dtype) for...  14.1 us
    ppermute x15, starting transfers between devices, around(): lax.ppermute(value, axis, [(k, (k + steps) % count) for k in range(count)])  13.5 us
    all_to_all x1, starting transfers between devices, layer(): arrived = lax.all_to_all(msg, CHIPS, 0, 0)  11.2 us
    ppermute x15, waiting for transfers between devices, around(): lax.ppermute(value, axis, [(k, (k + steps) % count) for k in range(count)])  9.46 us
    ppermute x2, starting transfers between devices, layer(): lax.ppermute(edge, SEQ, [(2 * k + 1, 2 * k + 2 + to) for k in range(chips...  7.09 us
    unnamed x16, local copies, waits for them, and re-layouts  3.22 us
  transfers between devices with their start and end apart: 18, of which 3 were waited for; matrix products, arithmetic and copies ran while one was open for 4% of the time, Pallas kernels for 10%

profile of v2, /device:TPU:1, one launch (start us, length us, event | category | flops | bytes accessed | tf_op | source)
XLA Modules:
  0.0 81.2 jit_solution(2730755875114702108)
XLA Ops:
  0.0 3.2 %collective-permute-start = (bf16[2,256,512]{2,1,0:T(8,128)(2,1)}, bf16[2,256,512]{2,1,0:T(8,128)(2,1)S(1)}, u32[]{:S(2)}, u32[]{:S(2)}) collective-permute-start(bf16[2,256,512]{2,1,0:T(8,128)(2,1)} %tokens_ref.1), channel_id=1, source_target_pairs={{0,4},{4,0},{1,5},{5,1},{2,6},{6,2},{3,7},{7,3},{8,12},{12,8},{9,1... | collective-permute-start | bytes 1572872 | tf_op jit(solution)/shard_map/ppermute | solution.py:302
  3.2 0.7 broadcast_in_dim.15
  3.9 0.1 broadcast_in_dim_reshape.3
  4.0 0.7 broadcast_in_dim.14
  4.7 0.7 pad_add_fusion.2.prm_ref.own_prm_ref
  5.4 1.0 %slice_select_fusion.2 = bf16[256,256]{1,0:T(8,128)(2,1)S(1)} fusion(bf16[512,256]{1,0:T(8,128)(2,1)} %w_ref.1, pred[]{:T(512)S(6)} %eq.3), kind=kLoop, calls=%fused_computation.4 | loop fusion | flops 65536 | bytes 393217 | tf_op jit(solution)/shard_map/jit(_where)/select_n | solution.py:331
  6.4 0.0 copy-start.5
  6.4 0.8 %collective-permute-start.6 = (bf16[272,256]{1,0:T(8,128)(2,1)S(1)}, bf16[272,256]{1,0:T(8,128)(2,1)S(1)}, u32[]{:S(2)}, u32[]{:S(2)}) collective-permute-start(bf16[272,256]{1,0:T(8,128)(2,1)S(1)} %pad_add_fusion.1), channel_id=1, source_target_pairs={{0,3},{1,0},{2,1},{3,2},{4,7},{5,4},{6,5},{7,6},{8,11},{9,8},{10,9... | collective-permute-start | bytes 417800 | tf_op jit(solution)/shard_map/ppermute | solution.py:302
  7.3 0.5 collective-permute-start.5
  7.8 0.6 collective-permute-start.4
  8.4 0.9 %collective-permute-start.1 = (bf16[2,16,256]{2,1,0:T(8,128)(2,1)S(1)}, bf16[2,16,256]{2,1,0:T(8,128)(2,1)S(1)}, u32[]{:S(2)}, u32[]{:S(2)}) collective-permute-start(bf16[2,16,256]{2,1,0:T(8,128)(2,1)S(1)} %bitcast.3), channel_id=1, source_target_pairs={{0,4},{4,0},{1,5},{5,1},{2,6},{6,2},{3,7},{7,3},{8,12},{12,8},{9,1... | collective-permute-start | bytes 49160 | tf_op jit(solution)/shard_map/ppermute | solution.py:302
  9.3 0.8 %collective-permute-done.1.got_log_ref = bf16[2,16,256]{2,1,0:T(8,128)(2,1)S(1)} collective-permute-done((bf16[2,16,256]{2,1,0:T(8,128)(2,1)S(1)}, bf16[2,16,256]{2,1,0:T(8,128)(2,1)S(1)}, u32[]{:S(2)}, u32[]{:S(2)}) %collective-permute-start.1) | collective-permute-done | bytes 16416 | tf_op jit(solution)/shard_map/ppermute | solution.py:302
  10.1 3.2 %collective-permute-start.3 = (bf16[2,16,512]{2,1,0:T(8,128)(2,1)S(1)}, bf16[2,16,512]{2,1,0:T(8,128)(2,1)S(1)}, u32[]{:S(2)}, u32[]{:S(2)}) collective-permute-start(bf16[2,16,512]{2,1,0:T(8,128)(2,1)S(1)} %slice.27), channel_id=1, source_target_pairs={{4,12},{12,20},{20,28},{28,36},{36,44},{44,52},{52,60},{60,68},{68... | collective-permute-start | bytes 98312 | tf_op jit(solution)/shard_map/ppermute | solution.py:337
  13.3 3.9 %collective-permute-start.2 = (bf16[2,16,512]{2,1,0:T(8,128)(2,1)S(1)}, bf16[2,16,512]{2,1,0:T(8,128)(2,1)S(1)}, u32[]{:S(2)}, u32[]{:S(2)}) collective-permute-start(bf16[2,16,512]{2,1,0:T(8,128)(2,1)S(1)} %slice.27), channel_id=1, source_target_pairs={{4,8},{12,16},{20,24},{28,32},{36,40},{44,48},{52,56},{60,64},{68,... | collective-permute-start | bytes 98312 | tf_op jit(solution)/shard_map/ppermute | solution.py:337
  17.3 0.0 collective-permute-done.5.rest_1_
  17.3 0.1 collective-permute-start.9
  17.4 0.5 collective-permute-start.8
  17.9 0.0 collective-permute-done.got_ref
  17.9 0.1 collective-permute-start.7
  18.0 0.9 %shard_map.100 = (bf16[512,512]{1,0:T(8,128)(2,1)S(1)}, bf16[512,128]{1,0:T(8,128)(2,1)S(1)}, bf16[512,128]{1,0:T(8,128)(2,1)S(1)}, bf16[8,1024]{1,0:T(8,128)(2,1)S(1)}) custom-call(s32[1]{0:T(128)} %bitcast.c_ref, s32[1]{0:T(128)} %bitcast.1.x_ref, bf16[2,256,512]{2,1,0:T(8,128)(2,1)S(1)} %copy-done.3, bf16[2,16,256]{2,1,0:T(8,128)(2,1)S(1)} %bitcast.4, ...), custom_call_target="tpu_custom_call" | custom-call | flops 1000000000 | bytes 1048576 | tf_op jit(solution)/shard_map/pallas_call | solution.py:289
  18.9 0.0 collective-permute-done.3.h1_ref
  18.9 0.1 copy-done
  18.9 0.0 copy-done.4
  19.0 1.0 %shard_map.101 = (bf16[16,512]{1,0:T(8,128)(2,1)S(1)}, bf16[512,128]{1,0:T(8,128)(2,1)S(1)}, bf16[128,512]{1,0:T(8,128)(2,1)S(1)}, bf16[512,256]{1,0:T(8,128)(2,1)S(1)}, bf16[32,24,128]{2,1,0:T(8,128)(2,1)S(1)}) custom-call(s32[1]{0:T(128)} %bitcast.c_ref, bf16[512,512]{1,0:T(8,128)(2,1)S(1)} %get-tuple-element.29.tok_ref, ...), custom_call_target="tpu_custom_call" | custom-call | flops 1000000000 | bytes 1048576 | tf_op jit(solution)/shard_map/pallas_call | solution.py:289
  20.0 0.0 collective-permute-done.8.rest_4_
  20.0 0.0 collective-permute-done.7.rest_3_
  20.0 2.6 %shard_map.102 = (bf16[512,768]{1,0:T(8,128)(2,1)S(1)}, bf16[32,24,128]{2,1,0:T(8,128)(2,1)}, bf16[512,256]{1,0:T(8,128)(2,1)S(1)}, bf16[8,1024]{1,0:T(8,128)(2,1)S(1)}) custom-call(s32[1]{0:T(128)} %bitcast.c_ref, bf16[512,512]{1,0:T(8,128)(2,1)S(1)} %get-tuple-element.29.tok_ref, bf16[16,512]{1,0:T(8,128)(2,1)S(1)} %get-tuple-element.32.halo_ref, ...), custom_call_target="tpu_custom_call" | custom-call | flops 1000000000 | bytes 1048576 | tf_op jit(solution)/shard_map/pallas_call | solution.py:289
  22.7 11.2 %all-to-all-start = ((bf16[32,24,128]{2,1,0:T(8,128)(2,1)}), bf16[32,24,128]{2,1,0:T(8,128)(2,1)S(1)}, u32[]{:S(2)}, u32[]{:S(2)}) async-start(bf16[32,24,128]{2,1,0:T(8,128)(2,1)} %get-tuple-element.37), calls=%async_computation | async-start | bytes 393216 | tf_op jit(solution)/shard_map/all_to_all | solution.py:372
  33.9 0.0 copy-start.2
  34.0 0.9 %copy-done.2 = bf16[256,512]{1,0:T(8,128)(2,1)S(1)} copy-done((bf16[256,512]{1,0:T(8,128)(2,1)S(1)}, bf16[256,512]{1,0:T(8,128)(2,1)}, u32[]{:S(2)}) %copy-start.2) | copy-done | bytes 262168
  34.9 3.3 %collective-permute-start.12 = (bf16[512,256]{1,0:T(8,128)(2,1)S(1)}, bf16[512,256]{1,0:T(8,128)(2,1)S(1)}, u32[]{:S(2)}, u32[]{:S(2)}) collective-permute-start(bf16[512,256]{1,0:T(8,128)(2,1)S(1)} %pad_add_fusion), channel_id=1, source_target_pairs={{0,3},{1,0},{2,1},{3,2},{4,7},{5,4},{6,5},{7,6},{8,11},{9,8},{10,9... | collective-permute-start | bytes 786440 | tf_op jit(solution)/shard_map/ppermute | solution.py:302
  38.2 0.0 collective-permute-start.11
  38.2 0.7 collective-permute-start.10
  38.9 4.5 %shard_map.103.y_ref = bf16[512,1024]{1,0:T(8,128)(2,1)S(1)} custom-call(bf16[512,256]{1,0:T(8,128)(2,1)S(1)} %get-tuple-element.40.xa0_ref, bf16[512,768]{1,0:T(8,128)(2,1)S(1)} %get-tuple-element.41.xa1_ref, bf16[512,256]{1,0:T(8,128)(2,1)S(1)} %get-tuple-element.42.seen_ref, bf16[8,1024]{1,0:T(8,128)(2,1)S(1)} %get-tuple-element.43.prm_ref.gain_ref), custom_call_target="tpu_custom_call" | custom-call | flops 2000000000 | bytes 1048576 | tf_op jit(solution)/shard_map/pallas_call | solution.py:289
  43.4 1.0 %copy-done.6 = bf16[512,1024]{1,0:T(8,128)(2,1)} copy-done((bf16[512,1024]{1,0:T(8,128)(2,1)}, bf16[512,1024]{1,0:T(8,128)(2,1)S(1)}, u32[]{:S(2)}) %copy-start.6) | copy-done | bytes 1048600
  44.4 1.3 %collective-permute-done.11.rest_1_ = bf16[512,256]{1,0:T(8,128)(2,1)S(1)} collective-permute-done((bf16[512,256]{1,0:T(8,128)(2,1)S(1)}, bf16[512,256]{1,0:T(8,128)(2,1)S(1)}, u32[]{:S(2)}, u32[]{:S(2)}) %collective-permute-start.11) | collective-permute-done | bytes 262176 | tf_op jit(solution)/shard_map/ppermute | solution.py:302
  45.7 7.3 %collective-permute-done.10.rest_0_ = bf16[512,256]{1,0:T(8,128)(2,1)S(1)} collective-permute-done((bf16[512,256]{1,0:T(8,128)(2,1)S(1)}, bf16[512,256]{1,0:T(8,128)(2,1)S(1)}, u32[]{:S(2)}, u32[]{:S(2)}) %collective-permute-start.10) | collective-permute-done | bytes 262176 | tf_op jit(solution)/shard_map/ppermute | solution.py:302
  53.0 0.8 collective-permute-start.13
  53.8 0.0 collective-permute-start.14
  53.8 0.5 collective-permute-start.15
  54.3 0.1 shard_map.104
  54.4 18.9 %all_to_all.10.back_ref = bf16[32,16,128]{2,1,0:T(8,128)(2,1)S(1)} all-to-all(bf16[32,16,128]{2,1,0:T(8,128)(2,1)S(1)} %shard_map.104), channel_id=1, replica_groups=mesh['seq_0'=8,'seq_1'=4,'seq_2'=2,'mix'=4] {'seq_0','seq_1'}, dimensions={0} | all-to-all | bytes 262144 | tf_op jit(solution)/shard_map/all_to_all | solution.py:383
  73.4 1.2 %copy-done.7 = bf16[512,1024]{1,0:T(8,128)(2,1)S(1)} copy-done((bf16[512,1024]{1,0:T(8,128)(2,1)S(1)}, bf16[512,1024]{1,0:T(8,128)(2,1)}, u32[]{:S(2)}) %copy-start.7) | copy-done | bytes 1048600
  74.6 1.4 %shard_map.105 = (bf16[512,1024]{1,0:T(8,128)(2,1)S(1)}, bf16[512,1024]{1,0:T(8,128)(2,1)S(1)}, bf16[1024,512]{1,0:T(8,128)(2,1)S(1)}) custom-call(s32[1]{0:T(128)} %bitcast.c_ref, bf16[512,512]{1,0:T(8,128)(2,1)S(1)} %get-tuple-element.29.tok_ref, bf16[512,256]{1,0:T(8,128)(2,1)S(1)} %get-tuple-element.42.seen_ref, bf16[512,1024]{1,0:T(8,128)(2,1)S(1)} %copy-done.7, ...), custom_call_target="tpu_custom_call" | custom-call | flops 2000000000 | bytes 1048576 | tf_op jit(solution)/shard_map/pallas_call | solution.py:289
  76.0 1.4 %shard_map.107 = bf16[256,512]{1,0:T(8,128)(2,1)S(1)} custom-call(s32[1]{0:T(128)} %bitcast.c_ref, bf16[32,16,128]{2,1,0:T(8,128)(2,1)S(1)} %all_to_all.10.back_ref, bf16[512,256]{1,0:T(8,128)(2,1)S(1)} %get-tuple-element.42.seen_ref, bf16[512,1024]{1,0:T(8,128)(2,1)S(1)} %get-tuple-element.50.yg_ref, bf16[512,1024]{1,0:T(8,128)(2,1)S(1)} %get-tuple-element.51.eg_ref, ...), custom_call_target="tpu_custom_call" | custom-call | flops 1000000000 | bytes 1048576 | tf_op jit(solution)/shard_map/pallas_call | solution.py:289
  77.3 1.5 %collective-permute-start.16 = (bf16[256,512]{1,0:T(8,128)(2,1)S(1)}, bf16[256,512]{1,0:T(8,128)(2,1)S(1)}, u32[]{:S(2)}, u32[]{:S(2)}) collective-permute-start(bf16[256,512]{1,0:T(8,128)(2,1)S(1)} %shard_map.107), channel_id=1, source_target_pairs={{0,4},{4,0},{1,5},{5,1},{2,6},{6,2},{3,7},{7,3},{8,12},{12,8},{9,1... | collective-permute-start | bytes 786440 | tf_op jit(solution)/shard_map/ppermute | solution.py:302
  78.9 1.4 %shard_map.106.own_ref = bf16[256,512]{1,0:T(8,128)(2,1)S(1)} custom-call(s32[1]{0:T(128)} %bitcast.c_ref, bf16[32,16,128]{2,1,0:T(8,128)(2,1)S(1)} %all_to_all.10.back_ref, bf16[512,256]{1,0:T(8,128)(2,1)S(1)} %get-tuple-element.42.seen_ref, bf16[512,1024]{1,0:T(8,128)(2,1)S(1)} %get-tuple-element.50.yg_ref, ...), custom_call_target="tpu_custom_call" | custom-call | flops 1000000000 | bytes 1048576 | tf_op jit(solution)/shard_map/pallas_call | solution.py:289
  80.2 0.8 shard_map.108
  (25 shorter events, 0.1 us)
Async XLA Ops:
  0.0 9.3 %copy-start.3 = (bf16[2,256,512]{2,1,0:T(8,128)(2,1)S(1)}, bf16[2,256,512]{2,1,0:T(8,128)(2,1)}, u32[]{:S(2)}) copy-start(bf16[2,256,512]{2,1,0:T(8,128)(2,1)} %tokens_ref.1) | copy-start | bytes 1572868
  0.0 17.9 %collective-permute-start = (bf16[2,256,512]{2,1,0:T(8,128)(2,1)}, bf16[2,256,512]{2,1,0:T(8,128)(2,1)S(1)}, u32[]{:S(2)}, u32[]{:S(2)}) collective-permute-start(bf16[2,256,512]{2,1,0:T(8,128)(2,1)} %tokens_ref.1), channel_id=1, source_target_pairs={{0,4},{4,0},{1,5},{5,1},{2,6},{6,2},{3,7},{7,3},{8,12},{12,8},{9,1... | collective-permute-start | bytes 1572872 | tf_op jit(solution)/shard_map/ppermute | solution.py:302
  6.4 2.0 %copy-start.5 = (bf16[2,256,16]{1,2,0:T(8,128)(2,1)S(1)}, bf16[2,256,16]{1,2,0:T(8,128)(2,1)}, u32[]{:S(2)}) copy-start(bf16[2,256,16]{1,2,0:T(8,128)(2,1)} %param.11) | copy-start | bytes 49156
  6.4 6.9 %collective-permute-start.6 = (bf16[272,256]{1,0:T(8,128)(2,1)S(1)}, bf16[272,256]{1,0:T(8,128)(2,1)S(1)}, u32[]{:S(2)}, u32[]{:S(2)}) collective-permute-start(bf16[272,256]{1,0:T(8,128)(2,1)S(1)} %pad_add_fusion.1), channel_id=1, source_target_pairs={{0,3},{1,0},{2,1},{3,2},{4,7},{5,4},{6,5},{7,6},{8,11},{9,8},{10,9... | collective-permute-start | bytes 417800 | tf_op jit(solution)/shard_map/ppermute | solution.py:302
  7.3 10.0 %collective-permute-start.5 = (bf16[272,256]{1,0:T(8,128)(2,1)S(1)}, bf16[272,256]{1,0:T(8,128)(2,1)S(1)}, u32[]{:S(2)}, u32[]{:S(2)}) collective-permute-start(bf16[272,256]{1,0:T(8,128)(2,1)S(1)} %pad_add_fusion.1), channel_id=1, source_target_pairs={{0,2},{1,3},{2,0},{3,1},{4,6},{5,7},{6,4},{7,5},{8,10},{9,11},{10,... | collective-permute-start | bytes 417800 | tf_op jit(solution)/shard_map/ppermute | solution.py:302
  7.8 9.6 %collective-permute-start.4 = (bf16[272,256]{1,0:T(8,128)(2,1)S(1)}, bf16[272,256]{1,0:T(8,128)(2,1)S(1)}, u32[]{:S(2)}, u32[]{:S(2)}) collective-permute-start(bf16[272,256]{1,0:T(8,128)(2,1)S(1)} %pad_add_fusion.1), channel_id=1, source_target_pairs={{0,1},{1,2},{2,3},{3,0},{4,5},{5,6},{6,7},{7,4},{8,9},{9,10},{10,1... | collective-permute-start | bytes 417800 | tf_op jit(solution)/shard_map/ppermute | solution.py:302
  8.4 1.7 %collective-permute-start.1 = (bf16[2,16,256]{2,1,0:T(8,128)(2,1)S(1)}, bf16[2,16,256]{2,1,0:T(8,128)(2,1)S(1)}, u32[]{:S(2)}, u32[]{:S(2)}) collective-permute-start(bf16[2,16,256]{2,1,0:T(8,128)(2,1)S(1)} %bitcast.3), channel_id=1, source_target_pairs={{0,4},{4,0},{1,5},{5,1},{2,6},{6,2},{3,7},{7,3},{8,12},{12,8},{9,1... | collective-permute-start | bytes 49160 | tf_op jit(solution)/shard_map/ppermute | solution.py:302
  10.1 8.7 %collective-permute-start.3 = (bf16[2,16,512]{2,1,0:T(8,128)(2,1)S(1)}, bf16[2,16,512]{2,1,0:T(8,128)(2,1)S(1)}, u32[]{:S(2)}, u32[]{:S(2)}) collective-permute-start(bf16[2,16,512]{2,1,0:T(8,128)(2,1)S(1)} %slice.27), channel_id=1, source_target_pairs={{4,12},{12,20},{20,28},{28,36},{36,44},{44,52},{52,60},{60,68},{68... | collective-permute-start | bytes 98312 | tf_op jit(solution)/shard_map/ppermute | solution.py:337
  13.3 5.5 %collective-permute-start.2 = (bf16[2,16,512]{2,1,0:T(8,128)(2,1)S(1)}, bf16[2,16,512]{2,1,0:T(8,128)(2,1)S(1)}, u32[]{:S(2)}, u32[]{:S(2)}) collective-permute-start(bf16[2,16,512]{2,1,0:T(8,128)(2,1)S(1)} %slice.27), channel_id=1, source_target_pairs={{4,8},{12,16},{20,24},{28,32},{36,40},{44,48},{52,56},{60,64},{68,... | collective-permute-start | bytes 98312 | tf_op jit(solution)/shard_map/ppermute | solution.py:337
  17.3 2.8 %collective-permute-start.9 = (bf16[272,256]{1,0:T(8,128)(2,1)S(1)}, bf16[272,256]{1,0:T(8,128)(2,1)S(1)}, u32[]{:S(2)}, u32[]{:S(2)}) collective-permute-start(bf16[272,256]{1,0:T(8,128)(2,1)S(1)} %collective-permute-done.6.rest_2_), channel_id=1, source_target_pairs={{0,4},{4,0},{1,5},{5,1},{2,6},{6,2},{3,7},{7,3},{8,12},{12,8},{9,1... | collective-permute-start | bytes 417800 | tf_op jit(solution)/shard_map/ppermute | solution.py:302
  17.4 2.6 %collective-permute-start.8 = (bf16[272,256]{1,0:T(8,128)(2,1)S(1)}, bf16[272,256]{1,0:T(8,128)(2,1)S(1)}, u32[]{:S(2)}, u32[]{:S(2)}) collective-permute-start(bf16[272,256]{1,0:T(8,128)(2,1)S(1)} %collective-permute-done.5.rest_1_), channel_id=1, source_target_pairs={{0,4},{4,0},{1,5},{5,1},{2,6},{6,2},{3,7},{7,3},{8,12},{12,8},{9,1... | collective-permute-start | bytes 417800 | tf_op jit(solution)/shard_map/ppermute | solution.py:302
  17.9 2.2 %collective-permute-start.7 = (bf16[272,256]{1,0:T(8,128)(2,1)S(1)}, bf16[272,256]{1,0:T(8,128)(2,1)S(1)}, u32[]{:S(2)}, u32[]{:S(2)}) collective-permute-start(bf16[272,256]{1,0:T(8,128)(2,1)S(1)} %collective-permute-done.4.rest_0_), channel_id=1, source_target_pairs={{0,4},{4,0},{1,5},{5,1},{2,6},{6,2},{3,7},{7,3},{8,12},{12,8},{9,1... | collective-permute-start | bytes 417800 | tf_op jit(solution)/shard_map/ppermute | solution.py:302
  18.0 0.9 %copy-start = (bf16[512,256]{1,0:T(8,128)(2,1)S(1)}, bf16[512,256]{1,0:T(8,128)(2,1)}, u32[]{:S(2)}) copy-start(bf16[512,256]{1,0:T(8,128)(2,1)} %w_ref.1) | copy-start | bytes 786436
  18.0 1.0 %copy-start.4 = (bf16[512,128]{1,0:T(8,128)(2,1)S(1)}, bf16[512,128]{1,0:T(8,128)(2,1)}, u32[]{:S(2)}) copy-start(bf16[512,128]{1,0:T(8,128)(2,1)} %wbc_ref.1) | copy-start | bytes 393220
  22.7 11.2 %copy-start.1 = (bf16[512,256]{1,0:T(8,128)(2,1)S(1)}, bf16[512,256]{1,0:T(8,128)(2,1)}, u32[]{:S(2)}) copy-start(bf16[512,256]{1,0:T(8,128)(2,1)} %wz0_ref) | copy-start | bytes 786436
  22.7 31.6 %all-to-all-start = ((bf16[32,24,128]{2,1,0:T(8,128)(2,1)}), bf16[32,24,128]{2,1,0:T(8,128)(2,1)S(1)}, u32[]{:S(2)}, u32[]{:S(2)}) async-start(bf16[32,24,128]{2,1,0:T(8,128)(2,1)} %get-tuple-element.37), calls=%async_computation | async-start | bytes 393216 | tf_op jit(solution)/shard_map/all_to_all | solution.py:372
  33.9 1.0 %copy-start.2 = (bf16[256,512]{1,0:T(8,128)(2,1)S(1)}, bf16[256,512]{1,0:T(8,128)(2,1)}, u32[]{:S(2)}) copy-start(bf16[256,512]{1,0:T(8,128)(2,1)} %wo0_ref) | copy-start | bytes 786436
  34.9 9.4 %collective-permute-start.12 = (bf16[512,256]{1,0:T(8,128)(2,1)S(1)}, bf16[512,256]{1,0:T(8,128)(2,1)S(1)}, u32[]{:S(2)}, u32[]{:S(2)}) collective-permute-start(bf16[512,256]{1,0:T(8,128)(2,1)S(1)} %pad_add_fusion), channel_id=1, source_target_pairs={{0,3},{1,0},{2,1},{3,2},{4,7},{5,4},{6,5},{7,6},{8,11},{9,8},{10,9... | collective-permute-start | bytes 786440 | tf_op jit(solution)/shard_map/ppermute | solution.py:302
  38.2 7.5 %collective-permute-start.11 = (bf16[512,256]{1,0:T(8,128)(2,1)S(1)}, bf16[512,256]{1,0:T(8,128)(2,1)S(1)}, u32[]{:S(2)}, u32[]{:S(2)}) collective-permute-start(bf16[512,256]{1,0:T(8,128)(2,1)S(1)} %pad_add_fusion), channel_id=1, source_target_pairs={{0,2},{1,3},{2,0},{3,1},{4,6},{5,7},{6,4},{7,5},{8,10},{9,11},{10,... | collective-permute-start | bytes 786440 | tf_op jit(solution)/shard_map/ppermute | solution.py:302
  38.2 14.8 %collective-permute-start.10 = (bf16[512,256]{1,0:T(8,128)(2,1)S(1)}, bf16[512,256]{1,0:T(8,128)(2,1)S(1)}, u32[]{:S(2)}, u32[]{:S(2)}) collective-permute-start(bf16[512,256]{1,0:T(8,128)(2,1)S(1)} %pad_add_fusion), channel_id=1, source_target_pairs={{0,1},{1,2},{2,3},{3,0},{4,5},{5,6},{6,7},{7,4},{8,9},{9,10},{10,1... | collective-permute-start | bytes 786440 | tf_op jit(solution)/shard_map/ppermute | solution.py:302
  43.4 1.0 %copy-start.6 = (bf16[512,1024]{1,0:T(8,128)(2,1)}, bf16[512,1024]{1,0:T(8,128)(2,1)S(1)}, u32[]{:S(2)}) copy-start(bf16[512,1024]{1,0:T(8,128)(2,1)S(1)} %shard_map.103.y_ref) | copy-start | bytes 3145732
  53.0 20.4 %collective-permute-start.13 = (bf16[512,256]{1,0:T(8,128)(2,1)S(1)}, bf16[512,256]{1,0:T(8,128)(2,1)S(1)}, u32[]{:S(2)}, u32[]{:S(2)}) collective-permute-start(bf16[512,256]{1,0:T(8,128)(2,1)S(1)} %collective-permute-done.10.rest_0_), channel_id=1, source_target_pairs={{0,4},{4,0},{1,5},{5,1},{2,6},{6,2},{3,7},{7,3},{8,12},{12,8},{9,1... | collective-permute-start | bytes 786440 | tf_op jit(solution)/shard_map/ppermute | solution.py:302
  53.8 19.6 %collective-permute-start.14 = (bf16[512,256]{1,0:T(8,128)(2,1)S(1)}, bf16[512,256]{1,0:T(8,128)(2,1)S(1)}, u32[]{:S(2)}, u32[]{:S(2)}) collective-permute-start(bf16[512,256]{1,0:T(8,128)(2,1)S(1)} %collective-permute-done.11.rest_1_), channel_id=1, source_target_pairs={{0,4},{4,0},{1,5},{5,1},{2,6},{6,2},{3,7},{7,3},{8,12},{12,8},{9,1... | collective-permute-start | bytes 786440 | tf_op jit(solution)/shard_map/ppermute | solution.py:302
  53.8 19.6 %collective-permute-start.15 = (bf16[512,256]{1,0:T(8,128)(2,1)S(1)}, bf16[512,256]{1,0:T(8,128)(2,1)S(1)}, u32[]{:S(2)}, u32[]{:S(2)}) collective-permute-start(bf16[512,256]{1,0:T(8,128)(2,1)S(1)} %collective-permute-done.12.rest_2_), channel_id=1, source_target_pairs={{0,4},{4,0},{1,5},{5,1},{2,6},{6,2},{3,7},{7,3},{8,12},{12,8},{9,1... | collective-permute-start | bytes 786440 | tf_op jit(solution)/shard_map/ppermute | solution.py:302
  73.4 1.2 %copy-start.7 = (bf16[512,1024]{1,0:T(8,128)(2,1)S(1)}, bf16[512,1024]{1,0:T(8,128)(2,1)}, u32[]{:S(2)}) copy-start(bf16[512,1024]{1,0:T(8,128)(2,1)} %copy-done.6) | copy-start | bytes 3145732
  77.3 2.9 %collective-permute-start.16 = (bf16[256,512]{1,0:T(8,128)(2,1)S(1)}, bf16[256,512]{1,0:T(8,128)(2,1)S(1)}, u32[]{:S(2)}, u32[]{:S(2)}) collective-permute-start(bf16[256,512]{1,0:T(8,128)(2,1)S(1)} %shard_map.107), channel_id=1, source_target_pairs={{0,4},{4,0},{1,5},{5,1},{2,6},{6,2},{3,7},{7,3},{8,12},{12,8},{9,1... | collective-permute-start | bytes 786440 | tf_op jit(solution)/shard_map/ppermute | solution.py:302

commit v3 on v2

--- a/solution.py
+++ b/solution.py
@@ -326,13 +326,14 @@
         padded(conv_x, 0, 16)
         + padded(gain[None], CONV, 16)
         + padded(jnp.repeat(skip, wide // skip.shape[0])[None], CONV + 1, 16)
-        + padded(conv_bc, 8, 16, wide)
-    )
-    first = padded(jnp.where(low, w_x[:half], w_x[half:]), 0, half + 16) + padded(extra, half, half + 16)
+    )
+    first = padded(jnp.where(low, w_x[:half], w_x[half:]), 0, half + 8) + padded(extra[:8], half, half + 8)
     x_here = [around(first, "mix", r) for r in (2, 1, 3)]
     x_here = [x_here[1], x_here[0], x_here[2]]
     got = around(tokens, "seq_2", 1)
     got_log = around(logs, "seq_2", 1)
+    own_taps, _ = lax.optimization_barrier((conv_bc, first))
+    own_extra = extra + padded(own_taps, 8, 16, wide)
     edge = tokens[:, length - HALO :]
     halo = [lax.ppermute(edge, SEQ, [(2 * k + 1, 2 * k + 2 + to) for k in range(chips - 1)]) for to in range(2)]
     tok, logp, tail, totals = call(
@@ -356,7 +357,7 @@
             ((both, wide), BF16),
             ((parts, PART + 8, LANES), BF16),
         ],
-        (core_s, tok, *halo, tail, totals, w_bc, w_x, extra),
+        (core_s, tok, *halo, tail, totals, w_bc, w_x, own_extra),
         [SMEM] + [VMEM] * 5 + [ANY] * 2 + [VMEM],
         flops=10**9,
     )

time: 81.6 us -> 81.9 us (level)
  local copies, waits for them, and re-layouts: 4.7 us -> 5.82 us
    unnamed x16 -> x26, local copies, waits for them, and re-layouts: 3.22 us -> 4.98 us
  transfers between devices with their start and end apart: 18 -> 18, of which waited for: 3 -> 3; matrix products, arithmetic and copies ran while one was open for 4% -> 2% of each run, Pallas kernels for 10% -> 10%
where the time goes in v3:
time: 81.9 us; the launch traced here: 81.5 us
  starting transfers between devices  31.7 us (39%)
  blocking collectives  18.9 us (23%)
  Pallas kernels  14 us (17%)
  waiting for transfers between devices  9.45 us (12%)
  local copies, waits for them, and re-layouts  5.82 us (7%)
  other arithmetic  1.13 us (1%)
    all_to_all x1, blocking collectives, layer(): back = lax.all_to_all(carries, CHIPS, 0, 0)  18.9 us
    pallas_call x9, Pallas kernels, call(): pl.pallas_call(kernel, out_shape=[jax.ShapeDtypeStruct(shape, dtype) for...  14 us
    ppermute x15, starting transfers between devices, around(): lax.ppermute(value, axis, [(k, (k + steps) % count) for k in range(count)])  13.5 us
    all_to_all x1, starting transfers between devices, layer(): arrived = lax.all_to_all(msg, CHIPS, 0, 0)  11.2 us
    ppermute x15, waiting for transfers between devices, around(): lax.ppermute(value, axis, [(k, (k + steps) % count) for k in range(count)])  9.44 us
    ppermute x2, starting transfers between devices, layer(): lax.ppermute(edge, SEQ, [(2 * k + 1, 2 * k + 2 + to) for k in range(chips...  6.96 us
    unnamed x26, local copies, waits for them, and re-layouts  4.98 us
  transfers between devices with their start and end apart: 18, of which 3 were waited for; matrix products, arithmetic and copies ran while one was open for 2% of the time, Pallas kernels for 10%

profile of v3, /device:TPU:1, one launch (start us, length us, event | category | flops | bytes accessed | tf_op | source)
XLA Modules:
  0.0 81.5 jit_solution(1802185554246535348)
XLA Ops:
  0.0 3.2 %collective-permute-start = (bf16[2,256,512]{2,1,0:T(8,128)(2,1)}, bf16[2,256,512]{2,1,0:T(8,128)(2,1)S(1)}, u32[]{:S(2)}, u32[]{:S(2)}) collective-permute-start(bf16[2,256,512]{2,1,0:T(8,128)(2,1)} %tokens_ref.1), channel_id=1, source_target_pairs={{0,4},{4,0},{1,5},{5,1},{2,6},{6,2},{3,7},{7,3},{8,12},{12,8},{9,1... | collective-permute-start | bytes 1572872 | tf_op jit(solution)/shard_map/ppermute | solution.py:302
  3.2 0.7 broadcast_in_dim.14
  3.9 0.1 broadcast_in_dim.15
  3.9 0.1 broadcast_in_dim_reshape.3
  4.0 0.5 copy-done.10
  4.6 0.0 copy-start.3
  4.6 0.6 copy-done.3
  5.2 1.0 %slice_select_fusion.2 = bf16[256,256]{1,0:T(8,128)(2,1)S(1)} fusion(bf16[512,256]{1,0:T(8,128)(2,1)} %w_ref.1, pred[]{:T(512)S(6)} %eq.3), kind=kLoop, calls=%fused_computation.4 | loop fusion | flops 65536 | bytes 393217 | tf_op jit(solution)/shard_map/jit(_where)/select_n | solution.py:330
  6.2 0.0 copy-start.7
  6.3 0.0 copy-start.11
  6.3 0.8 %collective-permute-start.6 = (bf16[264,256]{1,0:T(8,128)(2,1)S(1)}, bf16[264,256]{1,0:T(8,128)(2,1)S(1)}, u32[]{:S(2)}, u32[]{:S(2)}) collective-permute-start(bf16[264,256]{1,0:T(8,128)(2,1)S(1)} %pad_add_fusion.1), channel_id=1, source_target_pairs={{0,3},{1,0},{2,1},{3,2},{4,7},{5,4},{6,5},{7,6},{8,11},{9,8},{10,9... | collective-permute-start | bytes 405512 | tf_op jit(solution)/shard_map/ppermute | solution.py:302
  7.1 0.5 collective-permute-start.5
  7.6 0.6 collective-permute-start.4
  8.2 0.9 %collective-permute-start.1 = (bf16[2,16,256]{2,1,0:T(8,128)(2,1)S(1)}, bf16[2,16,256]{2,1,0:T(8,128)(2,1)S(1)}, u32[]{:S(2)}, u32[]{:S(2)}) collective-permute-start(bf16[2,16,256]{2,1,0:T(8,128)(2,1)S(1)} %bitcast.3), channel_id=1, source_target_pairs={{0,4},{4,0},{1,5},{5,1},{2,6},{6,2},{3,7},{7,3},{8,12},{12,8},{9,1... | collective-permute-start | bytes 49160 | tf_op jit(solution)/shard_map/ppermute | solution.py:302
  9.1 0.8 collective-permute-done.1.got_log_ref
  9.9 3.2 %collective-permute-start.3 = (bf16[2,16,512]{2,1,0:T(8,128)(2,1)S(1)}, bf16[2,16,512]{2,1,0:T(8,128)(2,1)S(1)}, u32[]{:S(2)}, u32[]{:S(2)}) collective-permute-start(bf16[2,16,512]{2,1,0:T(8,128)(2,1)S(1)} %slice.30), channel_id=1, source_target_pairs={{4,12},{12,20},{20,28},{28,36},{36,44},{44,52},{52,60},{60,68},{68... | collective-permute-start | bytes 98312 | tf_op jit(solution)/shard_map/ppermute | solution.py:338
  13.1 3.8 %collective-permute-start.2 = (bf16[2,16,512]{2,1,0:T(8,128)(2,1)S(1)}, bf16[2,16,512]{2,1,0:T(8,128)(2,1)S(1)}, u32[]{:S(2)}, u32[]{:S(2)}) collective-permute-start(bf16[2,16,512]{2,1,0:T(8,128)(2,1)S(1)} %slice.30), channel_id=1, source_target_pairs={{4,8},{12,16},{20,24},{28,32},{36,40},{44,48},{52,56},{60,64},{68,... | collective-permute-start | bytes 98312 | tf_op jit(solution)/shard_map/ppermute | solution.py:338
  16.9 0.0 collective-permute-done.5.rest_1_
  16.9 0.1 collective-permute-start.9
  17.0 0.5 collective-permute-start.8
  17.5 0.1 collective-permute-start.7
  17.7 0.9 %shard_map.100 = (bf16[512,512]{1,0:T(8,128)(2,1)S(1)}, bf16[512,128]{1,0:T(8,128)(2,1)S(1)}, bf16[512,128]{1,0:T(8,128)(2,1)S(1)}, bf16[8,1024]{1,0:T(8,128)(2,1)S(1)}) custom-call(s32[1]{0:T(128)} %bitcast.c_ref, s32[1]{0:T(128)} %bitcast.1.x_ref, bf16[2,256,512]{2,1,0:T(8,128)(2,1)S(1)} %copy-done.5, bf16[2,16,256]{2,1,0:T(8,128)(2,1)S(1)} %bitcast.4, ...), custom_call_target="tpu_custom_call" | custom-call | flops 1000000000 | bytes 1048576 | tf_op jit(solution)/shard_map/pallas_call | solution.py:289
  18.5 0.1 copy-done
  18.6 0.0 copy-done.6
  18.6 1.0 %shard_map.101 = (bf16[16,512]{1,0:T(8,128)(2,1)S(1)}, bf16[512,128]{1,0:T(8,128)(2,1)S(1)}, bf16[128,512]{1,0:T(8,128)(2,1)S(1)}, bf16[512,256]{1,0:T(8,128)(2,1)S(1)}, bf16[32,24,128]{2,1,0:T(8,128)(2,1)S(1)}) custom-call(s32[1]{0:T(128)} %bitcast.c_ref, bf16[512,512]{1,0:T(8,128)(2,1)S(1)} %get-tuple-element.30.tok_ref, ...), custom_call_target="tpu_custom_call" | custom-call | flops 1000000000 | bytes 1048576 | tf_op jit(solution)/shard_map/pallas_call | solution.py:289
  19.7 0.0 copy-start.4
  19.7 0.7 copy-done.4
  20.4 2.6 %shard_map.102 = (bf16[512,768]{1,0:T(8,128)(2,1)S(1)}, bf16[32,24,128]{2,1,0:T(8,128)(2,1)}, bf16[512,256]{1,0:T(8,128)(2,1)S(1)}, bf16[8,1024]{1,0:T(8,128)(2,1)S(1)}) custom-call(s32[1]{0:T(128)} %bitcast.c_ref, bf16[512,512]{1,0:T(8,128)(2,1)S(1)} %get-tuple-element.30.tok_ref, bf16[16,512]{1,0:T(8,128)(2,1)S(1)} %get-tuple-element.34.halo_ref, ...), custom_call_target="tpu_custom_call" | custom-call | flops 1000000000 | bytes 1048576 | tf_op jit(solution)/shard_map/pallas_call | solution.py:289
  23.0 11.2 %all-to-all-start = ((bf16[32,24,128]{2,1,0:T(8,128)(2,1)}), bf16[32,24,128]{2,1,0:T(8,128)(2,1)S(1)}, u32[]{:S(2)}, u32[]{:S(2)}) async-start(bf16[32,24,128]{2,1,0:T(8,128)(2,1)} %get-tuple-element.39), calls=%async_computation | async-start | bytes 393216 | tf_op jit(solution)/shard_map/all_to_all | solution.py:373
  34.2 0.0 copy-start.2
  34.3 0.9 %copy-done.2 = bf16[256,512]{1,0:T(8,128)(2,1)S(1)} copy-done((bf16[256,512]{1,0:T(8,128)(2,1)S(1)}, bf16[256,512]{1,0:T(8,128)(2,1)}, u32[]{:S(2)}) %copy-start.2) | copy-done | bytes 262168
  35.2 3.3 %collective-permute-start.12 = (bf16[512,256]{1,0:T(8,128)(2,1)S(1)}, bf16[512,256]{1,0:T(8,128)(2,1)S(1)}, u32[]{:S(2)}, u32[]{:S(2)}) collective-permute-start(bf16[512,256]{1,0:T(8,128)(2,1)S(1)} %pad_add_fusion), channel_id=1, source_target_pairs={{0,3},{1,0},{2,1},{3,2},{4,7},{5,4},{6,5},{7,6},{8,11},{9,8},{10,9... | collective-permute-start | bytes 786440 | tf_op jit(solution)/shard_map/ppermute | solution.py:302
  38.5 0.7 collective-permute-start.10
  39.2 4.5 %shard_map.103.y_ref = bf16[512,1024]{1,0:T(8,128)(2,1)S(1)} custom-call(bf16[512,256]{1,0:T(8,128)(2,1)S(1)} %get-tuple-element.42.xa0_ref, bf16[512,768]{1,0:T(8,128)(2,1)S(1)} %get-tuple-element.43.xa1_ref, bf16[512,256]{1,0:T(8,128)(2,1)S(1)} %get-tuple-element.44.seen_ref, bf16[8,1024]{1,0:T(8,128)(2,1)S(1)} %get-tuple-element.45.prm_ref.gain_ref), custom_call_target="tpu_custom_call" | custom-call | flops 2000000000 | bytes 1048576 | tf_op jit(solution)/shard_map/pallas_call | solution.py:289
  43.7 1.0 %copy-done.8 = bf16[512,1024]{1,0:T(8,128)(2,1)} copy-done((bf16[512,1024]{1,0:T(8,128)(2,1)}, bf16[512,1024]{1,0:T(8,128)(2,1)S(1)}, u32[]{:S(2)}) %copy-start.8) | copy-done | bytes 1048600
  44.7 1.3 %collective-permute-done.11.rest_1_ = bf16[512,256]{1,0:T(8,128)(2,1)S(1)} collective-permute-done((bf16[512,256]{1,0:T(8,128)(2,1)S(1)}, bf16[512,256]{1,0:T(8,128)(2,1)S(1)}, u32[]{:S(2)}, u32[]{:S(2)}) %collective-permute-start.11) | collective-permute-done | bytes 262176 | tf_op jit(solution)/shard_map/ppermute | solution.py:302
  46.0 7.3 %collective-permute-done.10.rest_0_ = bf16[512,256]{1,0:T(8,128)(2,1)S(1)} collective-permute-done((bf16[512,256]{1,0:T(8,128)(2,1)S(1)}, bf16[512,256]{1,0:T(8,128)(2,1)S(1)}, u32[]{:S(2)}, u32[]{:S(2)}) %collective-permute-start.10) | collective-permute-done | bytes 262176 | tf_op jit(solution)/shard_map/ppermute | solution.py:302
  53.3 0.8 collective-permute-start.13
  54.1 0.0 collective-permute-start.14
  54.1 0.5 collective-permute-start.15
  54.6 0.1 shard_map.104
  54.7 18.9 %all_to_all.10.back_ref = bf16[32,16,128]{2,1,0:T(8,128)(2,1)S(1)} all-to-all(bf16[32,16,128]{2,1,0:T(8,128)(2,1)S(1)} %shard_map.104), channel_id=1, replica_groups=mesh['seq_0'=8,'seq_1'=4,'seq_2'=2,'mix'=4] {'seq_0','seq_1'}, dimensions={0} | all-to-all | bytes 262144 | tf_op jit(solution)/shard_map/all_to_all | solution.py:384
  73.7 1.2 %copy-done.9 = bf16[512,1024]{1,0:T(8,128)(2,1)S(1)} copy-done((bf16[512,1024]{1,0:T(8,128)(2,1)S(1)}, bf16[512,1024]{1,0:T(8,128)(2,1)}, u32[]{:S(2)}) %copy-start.9) | copy-done | bytes 1048600
  74.9 1.4 %shard_map.105 = (bf16[512,1024]{1,0:T(8,128)(2,1)S(1)}, bf16[512,1024]{1,0:T(8,128)(2,1)S(1)}, bf16[1024,512]{1,0:T(8,128)(2,1)S(1)}) custom-call(s32[1]{0:T(128)} %bitcast.c_ref, bf16[512,512]{1,0:T(8,128)(2,1)S(1)} %get-tuple-element.30.tok_ref, bf16[512,256]{1,0:T(8,128)(2,1)S(1)} %get-tuple-element.44.seen_ref, bf16[512,1024]{1,0:T(8,128)(2,1)S(1)} %copy-done.9, ...), custom_call_target="tpu_custom_call" | custom-call | flops 2000000000 | bytes 1048576 | tf_op jit(solution)/shard_map/pallas_call | solution.py:289
  76.3 1.4 %shard_map.107 = bf16[256,512]{1,0:T(8,128)(2,1)S(1)} custom-call(s32[1]{0:T(128)} %bitcast.c_ref, bf16[32,16,128]{2,1,0:T(8,128)(2,1)S(1)} %all_to_all.10.back_ref, bf16[512,256]{1,0:T(8,128)(2,1)S(1)} %get-tuple-element.44.seen_ref, bf16[512,1024]{1,0:T(8,128)(2,1)S(1)} %get-tuple-element.52.yg_ref, bf16[512,1024]{1,0:T(8,128)(2,1)S(1)} %get-tuple-element.53.eg_ref, ...), custom_call_target="tpu_custom_call" | custom-call | flops 1000000000 | bytes 1048576 | tf_op jit(solution)/shard_map/pallas_call | solution.py:289
  77.7 1.5 %collective-permute-start.16 = (bf16[256,512]{1,0:T(8,128)(2,1)S(1)}, bf16[256,512]{1,0:T(8,128)(2,1)S(1)}, u32[]{:S(2)}, u32[]{:S(2)}) collective-permute-start(bf16[256,512]{1,0:T(8,128)(2,1)S(1)} %shard_map.107), channel_id=1, source_target_pairs={{0,4},{4,0},{1,5},{5,1},{2,6},{6,2},{3,7},{7,3},{8,12},{12,8},{9,1... | collective-permute-start | bytes 786440 | tf_op jit(solution)/shard_map/ppermute | solution.py:302
  79.2 1.4 %shard_map.106.own_ref = bf16[256,512]{1,0:T(8,128)(2,1)S(1)} custom-call(s32[1]{0:T(128)} %bitcast.c_ref, bf16[32,16,128]{2,1,0:T(8,128)(2,1)S(1)} %all_to_all.10.back_ref, bf16[512,256]{1,0:T(8,128)(2,1)S(1)} %get-tuple-element.44.seen_ref, bf16[512,1024]{1,0:T(8,128)(2,1)S(1)} %get-tuple-element.52.yg_ref, ...), custom_call_target="tpu_custom_call" | custom-call | flops 1000000000 | bytes 1048576 | tf_op jit(solution)/shard_map/pallas_call | solution.py:289
  80.6 0.8 shard_map.108
  (38 shorter events, 0.2 us)
Async XLA Ops:
  0.0 3.9 %copy-start.12 = (bf16[4]{0:T(256)(128)(2,1)S(1)}, bf16[4]{0:T(256)(128)(2,1)}, u32[]{:S(2)}) copy-start(bf16[4]{0:T(256)(128)(2,1)} %param.17) | copy-start | bytes 28
  0.0 17.5 %collective-permute-start = (bf16[2,256,512]{2,1,0:T(8,128)(2,1)}, bf16[2,256,512]{2,1,0:T(8,128)(2,1)S(1)}, u32[]{:S(2)}, u32[]{:S(2)}) collective-permute-start(bf16[2,256,512]{2,1,0:T(8,128)(2,1)} %tokens_ref.1), channel_id=1, source_target_pairs={{0,4},{4,0},{1,5},{5,1},{2,6},{6,2},{3,7},{7,3},{8,12},{12,8},{9,1... | collective-permute-start | bytes 1572872 | tf_op jit(solution)/shard_map/ppermute | solution.py:302
  3.9 0.7 copy-start.10
  4.6 0.6 copy-start.3
  5.2 1.1 %slice-start = ((bf16[16,256]{1,0:T(8,128)(2,1)}), bf16[8,256]{1,0:T(8,128)(2,1)S(1)}, s32[]{:S(2)}) async-start(bf16[16,256]{1,0:T(8,128)(2,1)} %copy-done.3), calls=%async_computation.2 | async-start | bytes 8192 | tf_op jit(solution)/shard_map/slice | solution.py:330
  5.2 4.0 %copy-start.5 = (bf16[2,256,512]{2,1,0:T(8,128)(2,1)S(1)}, bf16[2,256,512]{2,1,0:T(8,128)(2,1)}, u32[]{:S(2)}) copy-start(bf16[2,256,512]{2,1,0:T(8,128)(2,1)} %tokens_ref.1) | copy-start | bytes 1572868
  6.2 2.0 %copy-start.7 = (bf16[2,256,16]{1,2,0:T(8,128)(2,1)S(1)}, bf16[2,256,16]{1,2,0:T(8,128)(2,1)}, u32[]{:S(2)}) copy-start(bf16[2,256,16]{1,2,0:T(8,128)(2,1)} %param.11) | copy-start | bytes 49156
  6.3 2.8 %copy-start.11 = (bf16[4,128]{1,0:T(4,128)(2,1)S(1)}, bf16[4,128]{1,0:T(4,128)(2,1)}, u32[]{:S(2)}) copy-start(bf16[4,128]{1,0:T(4,128)(2,1)} %param.16) | copy-start | bytes 3076
  6.3 6.9 %collective-permute-start.6 = (bf16[264,256]{1,0:T(8,128)(2,1)S(1)}, bf16[264,256]{1,0:T(8,128)(2,1)S(1)}, u32[]{:S(2)}, u32[]{:S(2)}) collective-permute-start(bf16[264,256]{1,0:T(8,128)(2,1)S(1)} %pad_add_fusion.1), channel_id=1, source_target_pairs={{0,3},{1,0},{2,1},{3,2},{4,7},{5,4},{6,5},{7,6},{8,11},{9,8},{10,9... | collective-permute-start | bytes 405512 | tf_op jit(solution)/shard_map/ppermute | solution.py:302
  7.1 9.8 %collective-permute-start.5 = (bf16[264,256]{1,0:T(8,128)(2,1)S(1)}, bf16[264,256]{1,0:T(8,128)(2,1)S(1)}, u32[]{:S(2)}, u32[]{:S(2)}) collective-permute-start(bf16[264,256]{1,0:T(8,128)(2,1)S(1)} %pad_add_fusion.1), channel_id=1, source_target_pairs={{0,2},{1,3},{2,0},{3,1},{4,6},{5,7},{6,4},{7,5},{8,10},{9,11},{10,... | collective-permute-start | bytes 405512 | tf_op jit(solution)/shard_map/ppermute | solution.py:302
  7.6 9.4 %collective-permute-start.4 = (bf16[264,256]{1,0:T(8,128)(2,1)S(1)}, bf16[264,256]{1,0:T(8,128)(2,1)S(1)}, u32[]{:S(2)}, u32[]{:S(2)}) collective-permute-start(bf16[264,256]{1,0:T(8,128)(2,1)S(1)} %pad_add_fusion.1), channel_id=1, source_target_pairs={{0,1},{1,2},{2,3},{3,0},{4,5},{5,6},{6,7},{7,4},{8,9},{9,10},{10,1... | collective-permute-start | bytes 405512 | tf_op jit(solution)/shard_map/ppermute | solution.py:302
  8.2 1.7 %collective-permute-start.1 = (bf16[2,16,256]{2,1,0:T(8,128)(2,1)S(1)}, bf16[2,16,256]{2,1,0:T(8,128)(2,1)S(1)}, u32[]{:S(2)}, u32[]{:S(2)}) collective-permute-start(bf16[2,16,256]{2,1,0:T(8,128)(2,1)S(1)} %bitcast.3), channel_id=1, source_target_pairs={{0,4},{4,0},{1,5},{5,1},{2,6},{6,2},{3,7},{7,3},{8,12},{12,8},{9,1... | collective-permute-start | bytes 49160 | tf_op jit(solution)/shard_map/ppermute | solution.py:302
  9.9 8.6 %collective-permute-start.3 = (bf16[2,16,512]{2,1,0:T(8,128)(2,1)S(1)}, bf16[2,16,512]{2,1,0:T(8,128)(2,1)S(1)}, u32[]{:S(2)}, u32[]{:S(2)}) collective-permute-start(bf16[2,16,512]{2,1,0:T(8,128)(2,1)S(1)} %slice.30), channel_id=1, source_target_pairs={{4,12},{12,20},{20,28},{28,36},{36,44},{44,52},{52,60},{60,68},{68... | collective-permute-start | bytes 98312 | tf_op jit(solution)/shard_map/ppermute | solution.py:338
  13.1 5.4 %collective-permute-start.2 = (bf16[2,16,512]{2,1,0:T(8,128)(2,1)S(1)}, bf16[2,16,512]{2,1,0:T(8,128)(2,1)S(1)}, u32[]{:S(2)}, u32[]{:S(2)}) collective-permute-start(bf16[2,16,512]{2,1,0:T(8,128)(2,1)S(1)} %slice.30), channel_id=1, source_target_pairs={{4,8},{12,16},{20,24},{28,32},{36,40},{44,48},{52,56},{60,64},{68,... | collective-permute-start | bytes 98312 | tf_op jit(solution)/shard_map/ppermute | solution.py:338
  16.9 2.8 %collective-permute-start.9 = (bf16[264,256]{1,0:T(8,128)(2,1)S(1)}, bf16[264,256]{1,0:T(8,128)(2,1)S(1)}, u32[]{:S(2)}, u32[]{:S(2)}) collective-permute-start(bf16[264,256]{1,0:T(8,128)(2,1)S(1)} %collective-permute-done.6.rest_2_), channel_id=1, source_target_pairs={{0,4},{4,0},{1,5},{5,1},{2,6},{6,2},{3,7},{7,3},{8,12},{12,8},{9,1... | collective-permute-start | bytes 405512 | tf_op jit(solution)/shard_map/ppermute | solution.py:302
  17.0 2.7 %collective-permute-start.8 = (bf16[264,256]{1,0:T(8,128)(2,1)S(1)}, bf16[264,256]{1,0:T(8,128)(2,1)S(1)}, u32[]{:S(2)}, u32[]{:S(2)}) collective-permute-start(bf16[264,256]{1,0:T(8,128)(2,1)S(1)} %collective-permute-done.5.rest_1_), channel_id=1, source_target_pairs={{0,4},{4,0},{1,5},{5,1},{2,6},{6,2},{3,7},{7,3},{8,12},{12,8},{9,1... | collective-permute-start | bytes 405512 | tf_op jit(solution)/shard_map/ppermute | solution.py:302
  17.5 2.2 %collective-permute-start.7 = (bf16[264,256]{1,0:T(8,128)(2,1)S(1)}, bf16[264,256]{1,0:T(8,128)(2,1)S(1)}, u32[]{:S(2)}, u32[]{:S(2)}) collective-permute-start(bf16[264,256]{1,0:T(8,128)(2,1)S(1)} %collective-permute-done.4.rest_0_), channel_id=1, source_target_pairs={{0,4},{4,0},{1,5},{5,1},{2,6},{6,2},{3,7},{7,3},{8,12},{12,8},{9,1... | collective-permute-start | bytes 405512 | tf_op jit(solution)/shard_map/ppermute | solution.py:302
  17.6 0.9 %copy-start = (bf16[512,256]{1,0:T(8,128)(2,1)S(1)}, bf16[512,256]{1,0:T(8,128)(2,1)}, u32[]{:S(2)}) copy-start(bf16[512,256]{1,0:T(8,128)(2,1)} %w_ref.1) | copy-start | bytes 786436
  17.7 1.0 %copy-start.6 = (bf16[512,128]{1,0:T(8,128)(2,1)S(1)}, bf16[512,128]{1,0:T(8,128)(2,1)}, u32[]{:S(2)}) copy-start(bf16[512,128]{1,0:T(8,128)(2,1)} %wbc_ref.1) | copy-start | bytes 393220
  19.7 0.7 copy-start.4
  23.0 11.2 %copy-start.1 = (bf16[512,256]{1,0:T(8,128)(2,1)S(1)}, bf16[512,256]{1,0:T(8,128)(2,1)}, u32[]{:S(2)}) copy-start(bf16[512,256]{1,0:T(8,128)(2,1)} %wz0_ref) | copy-start | bytes 786436
  23.0 31.6 %all-to-all-start = ((bf16[32,24,128]{2,1,0:T(8,128)(2,1)}), bf16[32,24,128]{2,1,0:T(8,128)(2,1)S(1)}, u32[]{:S(2)}, u32[]{:S(2)}) async-start(bf16[32,24,128]{2,1,0:T(8,128)(2,1)} %get-tuple-element.39), calls=%async_computation | async-start | bytes 393216 | tf_op jit(solution)/shard_map/all_to_all | solution.py:373
  34.2 1.0 %copy-start.2 = (bf16[256,512]{1,0:T(8,128)(2,1)S(1)}, bf16[256,512]{1,0:T(8,128)(2,1)}, u32[]{:S(2)}) copy-start(bf16[256,512]{1,0:T(8,128)(2,1)} %wo0_ref) | copy-start | bytes 786436
  35.2 9.4 %collective-permute-start.12 = (bf16[512,256]{1,0:T(8,128)(2,1)S(1)}, bf16[512,256]{1,0:T(8,128)(2,1)S(1)}, u32[]{:S(2)}, u32[]{:S(2)}) collective-permute-start(bf16[512,256]{1,0:T(8,128)(2,1)S(1)} %pad_add_fusion), channel_id=1, source_target_pairs={{0,3},{1,0},{2,1},{3,2},{4,7},{5,4},{6,5},{7,6},{8,11},{9,8},{10,9... | collective-permute-start | bytes 786440 | tf_op jit(solution)/shard_map/ppermute | solution.py:302
  38.5 7.5 %collective-permute-start.11 = (bf16[512,256]{1,0:T(8,128)(2,1)S(1)}, bf16[512,256]{1,0:T(8,128)(2,1)S(1)}, u32[]{:S(2)}, u32[]{:S(2)}) collective-permute-start(bf16[512,256]{1,0:T(8,128)(2,1)S(1)} %pad_add_fusion), channel_id=1, source_target_pairs={{0,2},{1,3},{2,0},{3,1},{4,6},{5,7},{6,4},{7,5},{8,10},{9,11},{10,... | collective-permute-start | bytes 786440 | tf_op jit(solution)/shard_map/ppermute | solution.py:302
  38.5 14.8 %collective-permute-start.10 = (bf16[512,256]{1,0:T(8,128)(2,1)S(1)}, bf16[512,256]{1,0:T(8,128)(2,1)S(1)}, u32[]{:S(2)}, u32[]{:S(2)}) collective-permute-start(bf16[512,256]{1,0:T(8,128)(2,1)S(1)} %pad_add_fusion), channel_id=1, source_target_pairs={{0,1},{1,2},{2,3},{3,0},{4,5},{5,6},{6,7},{7,4},{8,9},{9,10},{10,1... | collective-permute-start | bytes 786440 | tf_op jit(solution)/shard_map/ppermute | solution.py:302
  43.7 1.0 %copy-start.8 = (bf16[512,1024]{1,0:T(8,128)(2,1)}, bf16[512,1024]{1,0:T(8,128)(2,1)S(1)}, u32[]{:S(2)}) copy-start(bf16[512,1024]{1,0:T(8,128)(2,1)S(1)} %shard_map.103.y_ref) | copy-start | bytes 3145732
  53.3 20.4 %collective-permute-start.13 = (bf16[512,256]{1,0:T(8,128)(2,1)S(1)}, bf16[512,256]{1,0:T(8,128)(2,1)S(1)}, u32[]{:S(2)}, u32[]{:S(2)}) collective-permute-start(bf16[512,256]{1,0:T(8,128)(2,1)S(1)} %collective-permute-done.10.rest_0_), channel_id=1, source_target_pairs={{0,4},{4,0},{1,5},{5,1},{2,6},{6,2},{3,7},{7,3},{8,12},{12,8},{9,1... | collective-permute-start | bytes 786440 | tf_op jit(solution)/shard_map/ppermute | solution.py:302
  54.1 19.6 %collective-permute-start.14 = (bf16[512,256]{1,0:T(8,128)(2,1)S(1)}, bf16[512,256]{1,0:T(8,128)(2,1)S(1)}, u32[]{:S(2)}, u32[]{:S(2)}) collective-permute-start(bf16[512,256]{1,0:T(8,128)(2,1)S(1)} %collective-permute-done.11.rest_1_), channel_id=1, source_target_pairs={{0,4},{4,0},{1,5},{5,1},{2,6},{6,2},{3,7},{7,3},{8,12},{12,8},{9,1... | collective-permute-start | bytes 786440 | tf_op jit(solution)/shard_map/ppermute | solution.py:302
  54.1 19.6 %collective-permute-start.15 = (bf16[512,256]{1,0:T(8,128)(2,1)S(1)}, bf16[512,256]{1,0:T(8,128)(2,1)S(1)}, u32[]{:S(2)}, u32[]{:S(2)}) collective-permute-start(bf16[512,256]{1,0:T(8,128)(2,1)S(1)} %collective-permute-done.12.rest_2_), channel_id=1, source_target_pairs={{0,4},{4,0},{1,5},{5,1},{2,6},{6,2},{3,7},{7,3},{8,12},{12,8},{9,1... | collective-permute-start | bytes 786440 | tf_op jit(solution)/shard_map/ppermute | solution.py:302
  73.7 1.2 %copy-start.9 = (bf16[512,1024]{1,0:T(8,128)(2,1)S(1)}, bf16[512,1024]{1,0:T(8,128)(2,1)}, u32[]{:S(2)}) copy-start(bf16[512,1024]{1,0:T(8,128)(2,1)} %copy-done.8) | copy-start | bytes 3145732
  77.7 2.9 %collective-permute-start.16 = (bf16[256,512]{1,0:T(8,128)(2,1)S(1)}, bf16[256,512]{1,0:T(8,128)(2,1)S(1)}, u32[]{:S(2)}, u32[]{:S(2)}) collective-permute-start(bf16[256,512]{1,0:T(8,128)(2,1)S(1)} %shard_map.107), channel_id=1, source_target_pairs={{0,4},{4,0},{1,5},{5,1},{2,6},{6,2},{3,7},{7,3},{8,12},{12,8},{9,1... | collective-permute-start | bytes 786440 | tf_op jit(solution)/shard_map/ppermute | solution.py:302
